TPU v7x, 128 devices: a whole 4x4x4 slice. The times are simulated.
128 devices in a mesh: gx: 4 (over z), gy: 16 (over y, x), gz: 2 (over core).
Axes of the slice: x: 4, y: 4, z: 4, core: 2. Of those that a mesh axis runs over, the one named last changes fastest.
Arguments:
- particles: float32 [8, 1048576], P(None, ('gx', 'gy', 'gz')), may hold values from -0.5 to 0.5
- dest_key: int32 [1048576], P(('gx', 'gy', 'gz')), may hold values from 0 to 127, as said below
- cell_a: int32 [1048576], P(('gx', 'gy', 'gz')), may hold values from 0 to 255
- cell_b: int32 [1048576], P(('gx', 'gy', 'gz')), may hold values from 0 to 127
- velocity: float32 [2, 1024, 4096], P(None, 'gx', ('gy', 'gz')), may hold values from -6 to 6
Outputs:
- binned: float32 [8, 4194304], P(None, ('gx', 'gy', 'gz'))
- binned_cell: int32 [4194304], P(('gx', 'gy', 'gz'))
Inputs may be any that keep to these rules, and one draw needn't show every extreme that they name: Of the particles of one device at most 256 have any one value of dest_key, and one device is named by exactly 256 particles of every device.
All inputs are finite; a program needn't handle non-finite values.
Results may differ from a plain program's by a relative error of at most 0.0003.
Values sent between devices are 32-bit elements; how exact they have to be, the bound alone decides.
A program may use at most 64 MiB of HBM per device.

v0:
```python
import math

import jax
import jax.numpy as jnp
from jax import lax
from jax.sharding import Mesh
from jax.sharding import PartitionSpec as P

GX_GY_GZ = ("gx", "gy_0", "gy_1", "gz")
GY_GZ = ("gy_0", "gy_1", "gz")


step_length = 0.5


def extended(x, sides, width):
    for axis, dim in sides:
        peers, length = (lax.axis_size(axis), x.shape[dim])
        up = [(i, (i + 1) % peers) for i in range(peers - 1)]
        down = [(j, i) for i, j in up]
        last = lax.slice_in_dim(x, length - width, length, axis=dim)
        initial = lax.slice_in_dim(x, 0, width, axis=dim)
        before = lax.ppermute(last, axis, up)
        after = lax.ppermute(initial, axis, down)
        x = jnp.concatenate([before, x, after], axis=dim)
    return x


def split_up(x, dim, peers):
    before, after = (x.shape[:dim], x.shape[dim + 1 :])
    return jnp.moveaxis(x.reshape(*before, peers, -1, *after), dim, 0)


def in_order(pieces, dim):
    pieces = jnp.moveaxis(pieces, 0, dim)
    lengths = pieces.shape
    return pieces.reshape(*lengths[:dim], lengths[dim] * lengths[dim + 1], *lengths[dim + 2 :])


def turned_blocks(pieces, axes, sequence):
    lengths = [lax.axis_size(a) for a in axes]
    pieces = pieces.reshape(*lengths, *pieces.shape[1:])
    for k in sequence:
        pieces = lax.all_to_all(pieces, axes[k], split_axis=k, concat_axis=k, tiled=True)
    return pieces.reshape(-1, *pieces.shape[len(axes) :])


def core_and_chips(x, groups, sequence, split_dim, concat_dim):
    peers = lax.axis_size(groups[0]) * lax.axis_size(groups[1])
    pieces = split_up(x, split_dim, peers)
    return in_order(turned_blocks(pieces, groups, sequence), concat_dim)


def quad_weights(frac):
    return (0.5 * frac * (frac - 1.0), 1.0 - frac * frac, 0.5 * frac * (frac + 1.0))


def counted_ranks(dest_key, owners):
    block_size = math.gcd(dest_key.shape[0], 1024)
    owner_ids = lax.iota(jnp.int32, owners)
    lower = (
        lax.iota(jnp.int32, block_size)[:, None] > lax.iota(jnp.int32, block_size)[None, :]
    ).astype(jnp.bfloat16)

    def rank_block(seen_counts, keys_block):
        one_hot = (keys_block[:, None] == owner_ids[None, :]).astype(jnp.float32)
        before = jnp.dot(lower, one_hot.astype(jnp.bfloat16), preferred_element_type=jnp.float32)
        block_ranks = jnp.sum((before + seen_counts[None, :]) * one_hot, axis=1)
        return (seen_counts + jnp.sum(one_hot, axis=0), block_ranks.astype(jnp.int32))

    start_counts = jnp.zeros((owners,), jnp.float32)
    unused, ranks = lax.scan(rank_block, start_counts, dest_key.reshape(-1, block_size))
    return ranks.reshape(-1)


def bucket_rows(payload, dest_key, ranking, owners, capacity):
    count = dest_key.shape[0]
    block_size = math.gcd(count, 1024)
    owner_ids = lax.iota(jnp.int32, owners)
    rank_ids = lax.iota(jnp.int32, capacity)
    rows = payload.shape[0]

    def add_block(total, index):
        start = index * block_size
        keys_block = lax.dynamic_slice_in_dim(dest_key, start, block_size, 0)
        ranks_block = lax.dynamic_slice_in_dim(ranking, start, block_size, 0)
        values = lax.dynamic_slice_in_dim(payload, start, block_size, 1)
        owner_hot = (keys_block[:, None] == owner_ids[None, :]).astype(jnp.float32)
        rank_hot = (ranks_block[:, None] == rank_ids[None, :]).astype(jnp.float32)
        spread = values[:, :, None] * rank_hot[None, :, :]
        placed = lax.dot_general(
            spread,
            owner_hot,
            (((1,), (0,)), ((), ())),
            precision=lax.Precision.HIGHEST,
            preferred_element_type=jnp.float32,
        )
        return (total + placed, None)

    start_total = jnp.zeros((rows, capacity, owners), jnp.float32)
    total, unused = lax.scan(
        add_block, start_total, jnp.arange(count // block_size, dtype=jnp.int32)
    )
    return jnp.transpose(total, (0, 2, 1))


def shards(particles, dest_key, cell_a, cell_b, velocity):
    owners = lax.axis_size(GX_GY_GZ)
    particle_count = particles.shape[1]
    capacity = 4 * particle_count // owners
    tile_height = velocity.shape[1]
    tile_width = velocity.shape[2]
    ranking = counted_ranks(dest_key, owners)
    cell_shifted = (cell_a * tile_width + cell_b + 1).astype(jnp.float32)
    payload = jnp.concatenate([particles, cell_shifted[None, :]], axis=0)
    placed = bucket_rows(payload, dest_key, ranking, owners, capacity)
    outgoing = jnp.concatenate([placed[0:8], placed[8:9] - 1.0], axis=0)
    padded = extended(velocity, (("gx", 1), (GY_GZ, 2)), 1)
    padded_width = tile_width + 2
    both_fields = jnp.concatenate([padded[0], padded[1]], axis=1)
    row_ids = lax.iota(jnp.int32, tile_height + 2)
    col_ids = lax.iota(jnp.int32, padded_width)

    def interpolate(arrived_block):
        cell_ids = arrived_block[8].astype(jnp.int32)
        is_live = cell_ids >= 0
        safe_ids = jnp.maximum(cell_ids, 0)
        node_row = safe_ids // tile_width
        node_col = safe_ids % tile_width
        weights_a = quad_weights(arrived_block[0])
        weights_b = quad_weights(arrived_block[1])
        row_weight = jnp.zeros((cell_ids.shape[0], tile_height + 2), jnp.float32)
        col_weight = jnp.zeros((cell_ids.shape[0], padded_width), jnp.float32)
        for shift in range(3):
            row_weight = row_weight + weights_a[shift][:, None] * (
                node_row[:, None] + shift == row_ids[None, :]
            ).astype(jnp.float32)
            col_weight = col_weight + weights_b[shift][:, None] * (
                node_col[:, None] + shift == col_ids[None, :]
            ).astype(jnp.float32)
        rows_mixed = jnp.dot(
            row_weight,
            both_fields,
            precision=lax.Precision.HIGHEST,
            preferred_element_type=jnp.float32,
        )
        speed_first = jnp.sum(rows_mixed[:, :padded_width] * col_weight, axis=1)
        speed_second = jnp.sum(rows_mixed[:, padded_width:] * col_weight, axis=1)
        speed = jnp.stack([speed_first, speed_second], axis=0)
        return jnp.where(is_live[None], step_length * speed, 0.0)

    arrived = core_and_chips(outgoing, (("gx", "gy_0", "gy_1"), "gz"), (1, 0), 1, 1)
    flat = arrived.reshape(9, -1)
    count = flat.shape[1]
    block_size = math.gcd(count, 2048)

    def one_block(index):
        return interpolate(lax.dynamic_slice_in_dim(flat, index * block_size, block_size, 1))

    displace = lax.map(one_block, jnp.arange(count // block_size, dtype=jnp.int32))
    displace = jnp.transpose(displace, (1, 0, 2)).reshape(2, count)
    advanced = jnp.concatenate([flat[0:2], flat[2:4] + displace, flat[4:8]], axis=0)
    cell_ids = flat[8].astype(jnp.int32)
    advanced, cell_rows = (
        advanced.reshape((8,) + arrived.shape[1:]),
        cell_ids.reshape((1,) + arrived.shape[1:]),
    )
    binned = advanced.reshape(8, -1)
    binned_cell = cell_rows.reshape(-1)
    return (binned, binned_cell)


def solution(mesh):
    split = Mesh(
        mesh.devices.reshape(mesh.shape["gx"], 4, 4, mesh.shape["gz"]), ("gx", "gy_0", "gy_1", "gz")
    )
    in_specs = (P(None, GX_GY_GZ), P(GX_GY_GZ), P(GX_GY_GZ), P(GX_GY_GZ), P(None, "gx", GY_GZ))
    out_specs = (P(None, GX_GY_GZ), P(GX_GY_GZ))
    return jax.shard_map(
        shards, mesh=split, in_specs=in_specs, out_specs=out_specs, check_vma=False
    )
```

profile of v0, /device:TPU:43, one launch (start us, length us, event | category | flops | bytes accessed | tf_op | source)
XLA Modules:
  0.0 259.1 jit_solution(3912188636909918199)
XLA Ops:
  1.5 7.5 %while.40 = (s32[]{:T(128)}, f32[128]{0:T(128)S(1)}, s32[8,1024]{1,0:T(8,128)S(1)}, s32[8,1024]{1,0:T(8,128)S(1)}, s32[]{:T(128)}, /*index=5*/s32[]{:T(128)}) while((s32[]{:T(128)}, f32[128]{0:T(128)S(1)}, s32[8,1024]{1,0:T(8,128)S(1)}, s32[8,1024]{1,0:T(8,128)S(1)}, s32[]{:T(128)}, /*index=5*/s32[]{:T(128)}) %tuple.104), condition=%wide.region_3.4_spmd.clone, body=%wide.region_0.3_spmd.clone.sunk | while | flops 271843456 | bytes 40023 | solution.py:72
  9.1 59.6 %while.41 = (s32[]{:T(128)}, f32[9,256,128]{2,1,0:T(8,128)S(1)}, s32[8]{0:T(128)S(1)}, f32[9,8192]{1,0:T(8,128)S(1)}, s32[8192]{0:T(1024)S(1)}, /*index=5*/s32[8...) while((s32[]{:T(128)}, f32[9,256,128]{2,1,0:T(8,128)S(1)}, s32[8]{0:T(128)S(1)}, ...), condition=%wide.region_5.6_spmd.clone, body=%wide.region_4.5_spmd.clone.sunk | while | flops 3627483136 | bytes 4591797 | solution.py:101
  26.2 5.3 %fusion.85 = f32[9,256,128]{2,1,0:T(8,128)S(1)} fusion(f32[1024,256]{0,1:T(8,128)S(1)} %fusion.84, f32[9,1024]{1,0:T(8,128)S(1)} %constant_dynamic-slice_fusion.6, f32[9,256,128]{2,1,0:T(8,128)S(1)} %get-tuple-element.513, pred[]{:T(512)S(6)} %compare.16, s32[1024]{0:T(1024)S(1)} %dynamic_slice.54), kind=kOutput, calls=%fused_computation.23.clone.1 | convolution fusion | flops 3626958848 | bytes 3448833 | tf_op jit(solution)/shard_map/while/body/eval_jaxpr/dot_general | solution.py:91
  41.1 5.3 %fusion.85 = f32[9,256,128]{2,1,0:T(8,128)S(1)} fusion(f32[1024,256]{0,1:T(8,128)S(1)} %fusion.84, f32[9,1024]{1,0:T(8,128)S(1)} %constant_dynamic-slice_fusion.6, f32[9,256,128]{2,1,0:T(8,128)S(1)} %get-tuple-element.513, pred[]{:T(512)S(6)} %compare.16, s32[1024]{0:T(1024)S(1)} %dynamic_slice.54), kind=kOutput, calls=%fused_computation.23.clone.1 | convolution fusion | flops 3626958848 | bytes 3448833 | tf_op jit(solution)/shard_map/while/body/eval_jaxpr/dot_general | solution.py:91
  63.4 5.3 %fusion.85 = f32[9,256,128]{2,1,0:T(8,128)S(1)} fusion(f32[1024,256]{0,1:T(8,128)S(1)} %fusion.84, f32[9,1024]{1,0:T(8,128)S(1)} %constant_dynamic-slice_fusion.6, f32[9,256,128]{2,1,0:T(8,128)S(1)} %get-tuple-element.513, pred[]{:T(512)S(6)} %compare.16, s32[1024]{0:T(1024)S(1)} %dynamic_slice.54), kind=kOutput, calls=%fused_computation.23.clone.1 | convolution fusion | flops 3626958848 | bytes 3448833 | tf_op jit(solution)/shard_map/while/body/eval_jaxpr/dot_general | solution.py:91
  78.4 10.5 %all-to-all-start.1 = ((f32[64,2,9,1,256]{4,3,2,1,0:T(1,128)}), f32[64,2,9,1,256]{4,3,2,1,0:T(1,128)S(1)}, u32[]{:S(2)}, u32[]{:S(2)}) async-start(f32[64,2,9,1,256]{4,3,2,1,0:T(1,128)} %copy.27), calls=%async_computation.1 | async-start | bytes 2359296 | tf_op jit(solution)/shard_map/all_to_all | solution.py:44
  97.7 10.0 %collective-permute-start.2 = (f32[2,258,1]{2,1,0:T(8,128)S(1)}, f32[2,258,1]{2,1,0:T(8,128)S(1)}, u32[]{:S(2)}, u32[]{:S(2)}) collective-permute-start(f32[2,258,1]{2,1,0:T(8,128)S(1)} %get-tuple-element.347), channel_id=1, source_target_pairs={{0,1},{1,2},{2,3},{3,4},{4,5},{5,6},{6,7},{7,8},{8,9},{9,10},{10,1... | collective-permute-start | bytes 6200 | tf_op jit(solution)/shard_map/ppermute | solution.py:23
  119.7 137.0 %while.39 = (s32[]{:T(128)}, f32[16,2,2048]{2,1,0:T(2,128)S(1)}, s32[16]{0:T(128)S(1)}, f32[9,32768]{1,0:T(8,128)S(1)}, f32[258,260]{1,0:T(8,128)}, /*index=5*/s...) while((s32[]{:T(128)}, f32[16,2,2048]{2,1,0:T(2,128)S(1)}, ...), condition=%wide.region_9.10_spmd.clone.clone, body=%wide.region_6.9_spmd.clone.clone.sunk | while | flops 1656059904 | bytes 4856059 | solution.py:160
  121.4 6.3 %fusion.76 = f32[2048,260]{0,1:T(8,128)S(1)} fusion(f32[258,260]{1,0:T(8,128)} %get-tuple-element.558, f32[2048]{0:T(1024)S(1)} %bitcast.130, s32[2048]{0:T(1024)S(1)} %broadcast_add_fusion.5, f32[2048]{0:T(1024)S(1)} %bitcast.129, s32[2048]{0:T(1024)S(1)} %get-tuple-element.461, f32[2048]{0:T(1024)S(1)} %bitcast.128, s32[2048]{0:T(1024)S(1)} %get-tuple-element.459), kind=kOutput, calls=%fused_computation.33.clone.1 | convolution fusion | flops 1652785152 | bytes 2447392 | tf_op jit(solution)/shard_map/while/body/eval_jaxpr/dot_general | solution.py:141
  129.9 6.3 %fusion.76 = f32[2048,260]{0,1:T(8,128)S(1)} fusion(f32[258,260]{1,0:T(8,128)} %get-tuple-element.558, f32[2048]{0:T(1024)S(1)} %bitcast.130, s32[2048]{0:T(1024)S(1)} %broadcast_add_fusion.5, f32[2048]{0:T(1024)S(1)} %bitcast.129, s32[2048]{0:T(1024)S(1)} %get-tuple-element.461, f32[2048]{0:T(1024)S(1)} %bitcast.128, s32[2048]{0:T(1024)S(1)} %get-tuple-element.459), kind=kOutput, calls=%fused_computation.33.clone.1 | convolution fusion | flops 1652785152 | bytes 2447392 | tf_op jit(solution)/shard_map/while/body/eval_jaxpr/dot_general | solution.py:141
  138.5 6.3 %fusion.76 = f32[2048,260]{0,1:T(8,128)S(1)} fusion(f32[258,260]{1,0:T(8,128)} %get-tuple-element.558, f32[2048]{0:T(1024)S(1)} %bitcast.130, s32[2048]{0:T(1024)S(1)} %broadcast_add_fusion.5, f32[2048]{0:T(1024)S(1)} %bitcast.129, s32[2048]{0:T(1024)S(1)} %get-tuple-element.461, f32[2048]{0:T(1024)S(1)} %bitcast.128, s32[2048]{0:T(1024)S(1)} %get-tuple-element.459), kind=kOutput, calls=%fused_computation.33.clone.1 | convolution fusion | flops 1652785152 | bytes 2447392 | tf_op jit(solution)/shard_map/while/body/eval_jaxpr/dot_general | solution.py:141
  147.1 6.3 %fusion.76 = f32[2048,260]{0,1:T(8,128)S(1)} fusion(f32[258,260]{1,0:T(8,128)} %get-tuple-element.558, f32[2048]{0:T(1024)S(1)} %bitcast.130, s32[2048]{0:T(1024)S(1)} %broadcast_add_fusion.5, f32[2048]{0:T(1024)S(1)} %bitcast.129, s32[2048]{0:T(1024)S(1)} %get-tuple-element.461, f32[2048]{0:T(1024)S(1)} %bitcast.128, s32[2048]{0:T(1024)S(1)} %get-tuple-element.459), kind=kOutput, calls=%fused_computation.33.clone.1 | convolution fusion | flops 1652785152 | bytes 2447392 | tf_op jit(solution)/shard_map/while/body/eval_jaxpr/dot_general | solution.py:141
  155.6 6.3 %fusion.76 = f32[2048,260]{0,1:T(8,128)S(1)} fusion(f32[258,260]{1,0:T(8,128)} %get-tuple-element.558, f32[2048]{0:T(1024)S(1)} %bitcast.130, s32[2048]{0:T(1024)S(1)} %broadcast_add_fusion.5, f32[2048]{0:T(1024)S(1)} %bitcast.129, s32[2048]{0:T(1024)S(1)} %get-tuple-element.461, f32[2048]{0:T(1024)S(1)} %bitcast.128, s32[2048]{0:T(1024)S(1)} %get-tuple-element.459), kind=kOutput, calls=%fused_computation.33.clone.1 | convolution fusion | flops 1652785152 | bytes 2447392 | tf_op jit(solution)/shard_map/while/body/eval_jaxpr/dot_general | solution.py:141
  164.2 6.3 %fusion.76 = f32[2048,260]{0,1:T(8,128)S(1)} fusion(f32[258,260]{1,0:T(8,128)} %get-tuple-element.558, f32[2048]{0:T(1024)S(1)} %bitcast.130, s32[2048]{0:T(1024)S(1)} %broadcast_add_fusion.5, f32[2048]{0:T(1024)S(1)} %bitcast.129, s32[2048]{0:T(1024)S(1)} %get-tuple-element.461, f32[2048]{0:T(1024)S(1)} %bitcast.128, s32[2048]{0:T(1024)S(1)} %get-tuple-element.459), kind=kOutput, calls=%fused_computation.33.clone.1 | convolution fusion | flops 1652785152 | bytes 2447392 | tf_op jit(solution)/shard_map/while/body/eval_jaxpr/dot_general | solution.py:141
  172.7 6.3 %fusion.76 = f32[2048,260]{0,1:T(8,128)S(1)} fusion(f32[258,260]{1,0:T(8,128)} %get-tuple-element.558, f32[2048]{0:T(1024)S(1)} %bitcast.130, s32[2048]{0:T(1024)S(1)} %broadcast_add_fusion.5, f32[2048]{0:T(1024)S(1)} %bitcast.129, s32[2048]{0:T(1024)S(1)} %get-tuple-element.461, f32[2048]{0:T(1024)S(1)} %bitcast.128, s32[2048]{0:T(1024)S(1)} %get-tuple-element.459), kind=kOutput, calls=%fused_computation.33.clone.1 | convolution fusion | flops 1652785152 | bytes 2447392 | tf_op jit(solution)/shard_map/while/body/eval_jaxpr/dot_general | solution.py:141
  181.3 6.3 %fusion.76 = f32[2048,260]{0,1:T(8,128)S(1)} fusion(f32[258,260]{1,0:T(8,128)} %get-tuple-element.558, f32[2048]{0:T(1024)S(1)} %bitcast.130, s32[2048]{0:T(1024)S(1)} %broadcast_add_fusion.5, f32[2048]{0:T(1024)S(1)} %bitcast.129, s32[2048]{0:T(1024)S(1)} %get-tuple-element.461, f32[2048]{0:T(1024)S(1)} %bitcast.128, s32[2048]{0:T(1024)S(1)} %get-tuple-element.459), kind=kOutput, calls=%fused_computation.33.clone.1 | convolution fusion | flops 1652785152 | bytes 2447392 | tf_op jit(solution)/shard_map/while/body/eval_jaxpr/dot_general | solution.py:141
  189.9 6.3 %fusion.76 = f32[2048,260]{0,1:T(8,128)S(1)} fusion(f32[258,260]{1,0:T(8,128)} %get-tuple-element.558, f32[2048]{0:T(1024)S(1)} %bitcast.130, s32[2048]{0:T(1024)S(1)} %broadcast_add_fusion.5, f32[2048]{0:T(1024)S(1)} %bitcast.129, s32[2048]{0:T(1024)S(1)} %get-tuple-element.461, f32[2048]{0:T(1024)S(1)} %bitcast.128, s32[2048]{0:T(1024)S(1)} %get-tuple-element.459), kind=kOutput, calls=%fused_computation.33.clone.1 | convolution fusion | flops 1652785152 | bytes 2447392 | tf_op jit(solution)/shard_map/while/body/eval_jaxpr/dot_general | solution.py:141
  198.4 6.3 %fusion.76 = f32[2048,260]{0,1:T(8,128)S(1)} fusion(f32[258,260]{1,0:T(8,128)} %get-tuple-element.558, f32[2048]{0:T(1024)S(1)} %bitcast.130, s32[2048]{0:T(1024)S(1)} %broadcast_add_fusion.5, f32[2048]{0:T(1024)S(1)} %bitcast.129, s32[2048]{0:T(1024)S(1)} %get-tuple-element.461, f32[2048]{0:T(1024)S(1)} %bitcast.128, s32[2048]{0:T(1024)S(1)} %get-tuple-element.459), kind=kOutput, calls=%fused_computation.33.clone.1 | convolution fusion | flops 1652785152 | bytes 2447392 | tf_op jit(solution)/shard_map/while/body/eval_jaxpr/dot_general | solution.py:141
  207.0 6.3 %fusion.76 = f32[2048,260]{0,1:T(8,128)S(1)} fusion(f32[258,260]{1,0:T(8,128)} %get-tuple-element.558, f32[2048]{0:T(1024)S(1)} %bitcast.130, s32[2048]{0:T(1024)S(1)} %broadcast_add_fusion.5, f32[2048]{0:T(1024)S(1)} %bitcast.129, s32[2048]{0:T(1024)S(1)} %get-tuple-element.461, f32[2048]{0:T(1024)S(1)} %bitcast.128, s32[2048]{0:T(1024)S(1)} %get-tuple-element.459), kind=kOutput, calls=%fused_computation.33.clone.1 | convolution fusion | flops 1652785152 | bytes 2447392 | tf_op jit(solution)/shard_map/while/body/eval_jaxpr/dot_general | solution.py:141
  215.5 6.3 %fusion.76 = f32[2048,260]{0,1:T(8,128)S(1)} fusion(f32[258,260]{1,0:T(8,128)} %get-tuple-element.558, f32[2048]{0:T(1024)S(1)} %bitcast.130, s32[2048]{0:T(1024)S(1)} %broadcast_add_fusion.5, f32[2048]{0:T(1024)S(1)} %bitcast.129, s32[2048]{0:T(1024)S(1)} %get-tuple-element.461, f32[2048]{0:T(1024)S(1)} %bitcast.128, s32[2048]{0:T(1024)S(1)} %get-tuple-element.459), kind=kOutput, calls=%fused_computation.33.clone.1 | convolution fusion | flops 1652785152 | bytes 2447392 | tf_op jit(solution)/shard_map/while/body/eval_jaxpr/dot_general | solution.py:141
  224.1 6.3 %fusion.76 = f32[2048,260]{0,1:T(8,128)S(1)} fusion(f32[258,260]{1,0:T(8,128)} %get-tuple-element.558, f32[2048]{0:T(1024)S(1)} %bitcast.130, s32[2048]{0:T(1024)S(1)} %broadcast_add_fusion.5, f32[2048]{0:T(1024)S(1)} %bitcast.129, s32[2048]{0:T(1024)S(1)} %get-tuple-element.461, f32[2048]{0:T(1024)S(1)} %bitcast.128, s32[2048]{0:T(1024)S(1)} %get-tuple-element.459), kind=kOutput, calls=%fused_computation.33.clone.1 | convolution fusion | flops 1652785152 | bytes 2447392 | tf_op jit(solution)/shard_map/while/body/eval_jaxpr/dot_general | solution.py:141
  232.7 6.3 %fusion.76 = f32[2048,260]{0,1:T(8,128)S(1)} fusion(f32[258,260]{1,0:T(8,128)} %get-tuple-element.558, f32[2048]{0:T(1024)S(1)} %bitcast.130, s32[2048]{0:T(1024)S(1)} %broadcast_add_fusion.5, f32[2048]{0:T(1024)S(1)} %bitcast.129, s32[2048]{0:T(1024)S(1)} %get-tuple-element.461, f32[2048]{0:T(1024)S(1)} %bitcast.128, s32[2048]{0:T(1024)S(1)} %get-tuple-element.459), kind=kOutput, calls=%fused_computation.33.clone.1 | convolution fusion | flops 1652785152 | bytes 2447392 | tf_op jit(solution)/shard_map/while/body/eval_jaxpr/dot_general | solution.py:141
  241.2 6.3 %fusion.76 = f32[2048,260]{0,1:T(8,128)S(1)} fusion(f32[258,260]{1,0:T(8,128)} %get-tuple-element.558, f32[2048]{0:T(1024)S(1)} %bitcast.130, s32[2048]{0:T(1024)S(1)} %broadcast_add_fusion.5, f32[2048]{0:T(1024)S(1)} %bitcast.129, s32[2048]{0:T(1024)S(1)} %get-tuple-element.461, f32[2048]{0:T(1024)S(1)} %bitcast.128, s32[2048]{0:T(1024)S(1)} %get-tuple-element.459), kind=kOutput, calls=%fused_computation.33.clone.1 | convolution fusion | flops 1652785152 | bytes 2447392 | tf_op jit(solution)/shard_map/while/body/eval_jaxpr/dot_general | solution.py:141
  249.8 6.3 %fusion.76 = f32[2048,260]{0,1:T(8,128)S(1)} fusion(f32[258,260]{1,0:T(8,128)} %get-tuple-element.558, f32[2048]{0:T(1024)S(1)} %bitcast.130, s32[2048]{0:T(1024)S(1)} %broadcast_add_fusion.5, f32[2048]{0:T(1024)S(1)} %bitcast.129, s32[2048]{0:T(1024)S(1)} %get-tuple-element.461, f32[2048]{0:T(1024)S(1)} %bitcast.128, s32[2048]{0:T(1024)S(1)} %get-tuple-element.459), kind=kOutput, calls=%fused_computation.33.clone.1 | convolution fusion | flops 1652785152 | bytes 2447392 | tf_op jit(solution)/shard_map/while/body/eval_jaxpr/dot_general | solution.py:141
  (273 shorter events, 102.3 us)
Async XLA Ops:
  1.4 7.6 %copy-start.2 = (s32[8192]{0:T(1024)S(1)}, s32[8192]{0:T(1024)}, u32[]{:S(2)}) copy-start(s32[8192]{0:T(1024)} %param.14) | copy-start | bytes 98308
  1.4 7.6 %copy-start.3 = (s32[8192]{0:T(1024)S(1)}, s32[8192]{0:T(1024)}, u32[]{:S(2)}) copy-start(s32[8192]{0:T(1024)} %param.13) | copy-start | bytes 98308
  1.5 7.6 %copy-start.1 = (f32[8,8192]{1,0:T(8,128)S(1)}, f32[8,8192]{1,0:T(8,128)}, u32[]{:S(2)}) copy-start(f32[8,8192]{1,0:T(8,128)} %param.11) | copy-start | bytes 786436
  78.4 10.5 %copy-start = (f32[2,256,128]{2,1,0:T(8,128)S(1)}, f32[2,256,128]{2,1,0:T(8,128)}, u32[]{:S(2)}) copy-start(f32[2,256,128]{2,1,0:T(8,128)} %param.15) | copy-start | bytes 786436
  78.4 38.3 %all-to-all-start.1 = ((f32[64,2,9,1,256]{4,3,2,1,0:T(1,128)}), f32[64,2,9,1,256]{4,3,2,1,0:T(1,128)S(1)}, u32[]{:S(2)}, u32[]{:S(2)}) async-start(f32[64,2,9,1,256]{4,3,2,1,0:T(1,128)} %copy.27), calls=%async_computation.1 | async-start | bytes 2359296 | tf_op jit(solution)/shard_map/all_to_all | solution.py:44
  88.9 7.1 %collective-permute-start = (f32[2,1,128]{2,1,0:T(1,128)S(1)}, f32[2,1,128]{2,1,0:T(1,128)S(1)}, u32[]{:S(2)}, u32[]{:S(2)}) collective-permute-start(f32[2,1,128]{2,1,0:T(1,128)S(1)} %get-tuple-element.349), channel_id=1, source_target_pairs={{0,32},{32,64},{64,96},{1,33},{33,65},{65,97},{2,34},{34,66},{66,9... | collective-permute-start | bytes 3080 | tf_op jit(solution)/shard_map/ppermute | solution.py:23
  92.2 5.4 %collective-permute-start.1 = (f32[2,1,128]{2,1,0:T(1,128)S(1)}, f32[2,1,128]{2,1,0:T(1,128)S(1)}, u32[]{:S(2)}, u32[]{:S(2)}) collective-permute-start(f32[2,1,128]{2,1,0:T(1,128)S(1)} %get-tuple-element.350), channel_id=1, source_target_pairs={{32,0},{64,32},{96,64},{33,1},{65,33},{97,65},{34,2},{66,34},{98,6... | collective-permute-start | bytes 3080 | tf_op jit(solution)/shard_map/ppermute | solution.py:24
  97.7 13.4 %collective-permute-start.2 = (f32[2,258,1]{2,1,0:T(8,128)S(1)}, f32[2,258,1]{2,1,0:T(8,128)S(1)}, u32[]{:S(2)}, u32[]{:S(2)}) collective-permute-start(f32[2,258,1]{2,1,0:T(8,128)S(1)} %get-tuple-element.347), channel_id=1, source_target_pairs={{0,1},{1,2},{2,3},{3,4},{4,5},{5,6},{6,7},{7,8},{8,9},{9,10},{10,1... | collective-permute-start | bytes 6200 | tf_op jit(solution)/shard_map/ppermute | solution.py:23
  107.7 7.8 %collective-permute-start.3 = (f32[2,258,1]{2,1,0:T(8,128)S(1)}, f32[2,258,1]{2,1,0:T(8,128)S(1)}, u32[]{:S(2)}, u32[]{:S(2)}) collective-permute-start(f32[2,258,1]{2,1,0:T(8,128)S(1)} %get-tuple-element.348), channel_id=1, source_target_pairs={{1,0},{2,1},{3,2},{4,3},{5,4},{6,5},{7,6},{8,7},{9,8},{10,9},{11,1... | collective-permute-start | bytes 6200 | tf_op jit(solution)/shard_map/ppermute | solution.py:24
where the time goes:
time: 261 us; the launch traced here: 259 us
  matrix products  149 us (57%)
  local copies, waits for them, and re-layouts  30.6 us (12%)
  starting transfers between devices  27.9 us (11%)
  other arithmetic  18.7 us (7%)
  loops' own time  18 us (7%)
  waiting for transfers between devices  8.94 us (3%)
  blocking collectives  4.98 us (2%)
    dot_general x16, matrix products, interpolate(): jnp.dot(row_weight, both_fields, precision=lax.Precision.HIGHEST, preferr...  101 us
    dot_general x8, matrix products, add_block(): lax.dot_general(spread, owner_hot, (((1,), (0,)), ((), ())), precision=la...  42.7 us
    ppermute x2, starting transfers between devices, extended(): before = lax.ppermute(last, axis, up)  13.2 us
    another operation x1, loops' own time, shards(): lax.map(one_block, jnp.arange(count // block_size, dtype=jnp.int32))  12 us
    dynamic_slice x16, local copies, waits for them, and re-layouts, shards(): lax.map(one_block, jnp.arange(count // block_size, dtype=jnp.int32))  10.7 us
    all_to_all x1, starting transfers between devices, turned_blocks(): lax.all_to_all(pieces, axes[k], split_axis=k, concat_axis=k, tiled=True)  10.5 us
    reduce_sum x16, other arithmetic, interpolate(): speed_first = jnp.sum(rows_mixed[:, :padded_width] * col_weight, axis=1)  8.71 us
    ppermute x2, waiting for transfers between devices, extended(): after = lax.ppermute(initial, axis, down)  5.91 us
  transfers between devices with their start and end apart: 5, of which 4 were waited for; matrix products, arithmetic and copies ran while one was open for 1% of the time, Pallas kernels for 0%

commit v1 on v0

v1 whole, which is shorter than its diff:
```python
import jax
import jax.numpy as jnp
from jax import lax
from jax.experimental import pallas as pl
from jax.experimental.pallas import tpu as pltpu
from jax.sharding import PartitionSpec as P

BF = jnp.bfloat16
F32 = jnp.float32
I32 = jnp.int32
NT = (((1,), (1,)), ((), ()))
AXES = ("gx", "gy", "gz")
MESH = pl.DeviceIdType.MESH


def dotf(a, b):
    return jnp.dot(a, b, preferred_element_type=F32)


def row256(ref, j):
    r = ref[pl.ds(2*j,2),:]
    return jnp.concatenate([r[0:1],r[1:2]],axis=1)

def bucket(part, dest, ca, cb, out, cells, oh, srt, csrt, acc, stv, sts, sem):
    nb=32
    iod=lax.broadcasted_iota(I32,(128,256),0).astype(F32).astype(BF)
    one=jnp.ones((),BF); zero=jnp.zeros((),BF)
    def onehot(j,S):
        d=row256(dest,j).astype(F32).astype(BF)
        o=jnp.where(iod==jnp.broadcast_to(d,(128,256)),one,zero)
        oh[j]=o
        return S+o
    S=lax.fori_loop(0,nb,onehot,jnp.zeros((128,256),BF),unroll=4)
    ones=jnp.ones((256,256),BF)
    tot=dotf(S,ones)
    low=(lax.broadcasted_iota(I32,(128,128),0)>lax.broadcasted_iota(I32,(128,128),1)).astype(F32).astype(BF)
    start=dotf(low,tot.astype(BF))
    diag=lax.broadcasted_iota(I32,(128,128),0)==lax.broadcasted_iota(I32,(128,128),1)
    srow=jnp.sum(jnp.where(diag,start[:,:128],0.),axis=0,keepdims=True)
    trow=jnp.sum(jnp.where(diag,tot[:,:128],0.),axis=0,keepdims=True)
    stv[0:1,:]=srow.astype(I32)
    stv[1:2,:]=trow.astype(I32)
    cp=pltpu.make_async_copy(stv,sts,sem)
    cp.start()
    up=(lax.broadcasted_iota(I32,(256,256),0)<lax.broadcasted_iota(I32,(256,256),1)).astype(F32).astype(BF)
    acc[...]=jnp.zeros_like(acc)
    iol=lax.broadcasted_iota(I32,(256,256),0).astype(F32).astype(BF)
    hrow=(lax.broadcasted_iota(I32,(256,256),0)//8).astype(F32).astype(BF)
    hrow32=lax.broadcasted_iota(I32,(32,256),0).astype(F32).astype(BF)
    UB=2
    def place(jj,base):
        tot=None
        for u in range(UB):
            j=jj*UB+u
            o=oh[j]
            before=dotf(o,up)
            cnt=dotf(o,ones)
            pos=jnp.sum(o.astype(F32)*(before+base),axis=0,keepdims=True)
            base=base+cnt
            hi=jnp.floor(pos*(1/256)); lo=pos-256*hi
            hib=jnp.broadcast_to(hi.astype(BF),(256,256)); lob=jnp.broadcast_to(lo.astype(BF),(256,256))
            lot=jnp.where(iol==lob,one,zero)
            v=part[:,pl.ds(pl.multiple_of(j*256,256),256)]
            vh=v.astype(BF); vl=(v-vh.astype(F32)).astype(BF)
            m=hrow==hib
            vh2=jnp.concatenate([vh]*32,axis=0)
            vl2=jnp.concatenate([vl]*32,axis=0)
            m32=hrow32==hib[:32]
            a=row256(ca,j).astype(F32).astype(BF); b=row256(cb,j).astype(F32).astype(BF)
            A=jnp.concatenate([jnp.where(m,vh2,zero),jnp.where(m,vl2,zero),
               jnp.where(m32,jnp.broadcast_to(a,(32,256)),zero),jnp.where(m32,jnp.broadcast_to(b,(32,256)),zero)],axis=0)
            x=lax.dot_general(A,lot,NT,preferred_element_type=F32)
            tot = x if tot is None else tot+x
        acc[...]+=tot
        return base
    lax.fori_loop(0,nb//UB,place,start)
    for h in range(32):
        srt[:,h*256:(h+1)*256]=acc[h*8:(h+1)*8]+acc[256+h*8:256+(h+1)*8]
    cc=acc[512:544]*128.+acc[544:576]
    for h in range(32):
        csrt[0:1,h*256:(h+1)*256]=cc[h:h+1]
    cp.wait()
    lane=lax.broadcasted_iota(I32,(8,128),1)
    lane1=lane[0:1]
    def expand(d,_):
        s=sts[0,d]; n=sts[1,d]
        al=pl.multiple_of((s//128)*128,128); sh=s%128
        rot=(128-sh)%128
        x=srt[:,pl.ds(al,384)]
        c=csrt[:,pl.ds(al,384)]
        rs=[pltpu.roll(x[:,128*i:128*(i+1)],rot,1) for i in range(3)]
        cs=[pltpu.roll(c[:,128*i:128*(i+1)],rot,1) for i in range(3)]
        keep=lane<128-sh
        for i in range(2):
            live=lane+128*i<n
            out[d,:,128*i:128*(i+1)]=jnp.where(live,jnp.where(keep,rs[i],rs[i+1]),0.)
            w=jnp.where(live,jnp.where(keep,cs[i],cs[i+1]),-1.)
            cells[d,:,128*i:128*(i+1)]=w[0:1]
        return _
    lax.fori_loop(0,128,expand,0,unroll=8)


def split(x):
    h=x.astype(BF); return h,(x-h.astype(F32)).astype(BF)
def weights(t):
    return 0.5*t*(t-1.), 1.-t*t, 0.5*t*(t+1.)
def setup(vel, halo, fh, fl, tab, masks):
    mu,md,ml,mr=masks
    lane=lax.broadcasted_iota(I32,(1,128),1)
    z8=jnp.zeros((8,256),F32)
    for c in range(2):
        ft=jnp.transpose(vel[c])
        lrow=halo[2][c:c+1,:]*ml
        rrow=halo[3][c:c+1,:]*mr
        e=jnp.concatenate([lrow,ft,rrow,jnp.zeros((6,256),F32)],axis=0)
        h,l=split(e)
        fh[c*136:(c+1)*136]=h; fl[c*136:(c+1)*136]=l
        rows=[]
        for (mid,lc,rc,m) in ((0,4,5,mu),(1,6,7,md)):
            r=halo[mid][c:c+1,:128]*m
            le=halo[lc][c:c+1,:128]*(m*ml); re=halo[rc][c:c+1,:128]*(m*mr)
            rows.append(jnp.where(lane==0,pltpu.roll(le,1,1),pltpu.roll(r,1,1)))
            rows.append(r)
            rows.append(jnp.where(lane==127,pltpu.roll(re,127,1),pltpu.roll(r,127,1)))
        tab[c]=jnp.concatenate(rows+[jnp.zeros((2,128),F32)],axis=0)
def interp(v, cell, fh, fl, tab):
    n=v.shape[1]
    zero=jnp.zeros((),BF)
    f=v[0:1]; g=v[1:2]
    live=cell>=0.
    cm=jnp.maximum(cell,0.)
    a=jnp.floor(cm*(1/128)); b=cm-128.*a
    wf=weights(f); wg=weights(g)
    ga=jnp.floor((a-1.)*(1/16)); oa=(a-1.)-16.*ga
    gab=jnp.broadcast_to(ga.astype(BF),(16,n))
    d=lax.broadcasted_iota(I32,(16,n),0).astype(F32).astype(BF)-jnp.broadcast_to(oa.astype(BF),(16,n))
    hl=[split(w) for w in wf]
    m0=d==0;m1=d==1;m2=d==2;q1=d==-15;q2=d==-14
    pats=[]
    for i in range(2):
        w=[jnp.broadcast_to(x[i],(16,n)) for x in hl]
        pats.append((jnp.where(m0,w[0],jnp.where(m1,w[1],jnp.where(m2,w[2],zero))),
                     jnp.where(q1,w[1],jnp.where(q2,w[2],zero))))
    ms=[gab==float(G) for G in range(-1,16)]
    W=[jnp.concatenate([jnp.where(ms[G+1],pa,jnp.where(ms[G],pb,zero)) for G in range(16)],axis=0) for pa,pb in pats]
    H=fh[...]; L=fl[...]
    R=dotf(H,W[0])+dotf(L,W[0])+dotf(H,W[1])
    gb=jnp.floor(b*(1/8)); ob=b-8.*gb
    gbb=jnp.broadcast_to(gb,(8,n))
    s8=lax.broadcasted_iota(I32,(8,n),0).astype(F32)
    d8=s8-ob
    pa=jnp.where(d8==0,wg[0],jnp.where(d8==1,wg[1],jnp.where(d8==2,wg[2],0.)))
    pb=jnp.where(d8==-7,wg[1],jnp.where(d8==-6,wg[2],0.))
    accA=[jnp.zeros((8,n),F32)]*2; accB=[jnp.zeros((8,n),F32)]*2
    mprev=None
    for G in range(17):
        m=gbb==float(G) if G<16 else None
        for c in range(2):
            r=R[c*136+8*G:c*136+8*G+8]
            if m is not None: accA[c]=jnp.where(m,r,accA[c])
            if mprev is not None: accB[c]=jnp.where(mprev,r,accB[c])
        mprev=m
    si=lax.broadcasted_iota(I32,(8,n),0)
    wj=jnp.where((si==0)|(si==3),wg[0],jnp.where((si==1)|(si==4),wg[1],wg[2]))
    up=jnp.where(a==0.,wf[0],0.); dn=jnp.where(a==255.,wf[2],0.)
    Pm=jnp.where(si<3,up,jnp.where(si<6,dn,0.))*wj
    bi=jnp.broadcast_to(b.astype(I32),(8,n))
    out=v
    for c in range(2):
        T=tab[c]
        corr=jnp.concatenate([jnp.take_along_axis(T,bi[:,128*i:128*(i+1)],axis=1) for i in range(n//128)],axis=1)
        sp=jnp.sum(pa*accA[c]+pb*accB[c]+Pm*corr,axis=0,keepdims=True)
        disp=jnp.where(live,0.5*sp,0.)
        out=out+jnp.where(si==2+c,disp,0.)
    return out
U = 4


def place_of(p):
    return (p // 32, (p % 32) // 2, p % 2)


def bucket_edges(vel, part, dest, ca, cb, out, cells, edges, *scratch):
    for c in range(2):
        zeros = jnp.zeros((1, 128), F32)
        edges[0, c : c + 1, :] = jnp.concatenate([vel[c, 0:1, :], zeros], axis=1)
        edges[1, c : c + 1, :] = jnp.concatenate([vel[c, 255:256, :], zeros], axis=1)
        turned = jnp.transpose(vel[c])
        edges[2, c : c + 1, :] = turned[0:1]
        edges[3, c : c + 1, :] = turned[127:128]
    bucket(part, dest, ca, cb, out, cells, *scratch)


def exchange(vel, edges, send, scell, out, cout, recv, rcell, halo, fh, fl, tab, ss, ra, rb, rh):
    gx = lax.axis_index("gx")
    col = lax.axis_index("gy") * 2 + lax.axis_index("gz")
    me = gx * 32 + col
    barrier = pltpu.get_barrier_semaphore()

    def greet(k, _):
        p = lax.rem(me + k, 128)
        pl.semaphore_signal(barrier, inc=1, device_id=place_of(p), device_id_type=MESH)
        return _

    lax.fori_loop(1, 128, greet, 0)
    recv[me] = send[me]
    rcell[me] = scell[me]
    pl.semaphore_wait(barrier, 127)

    def neighbour(da, db):
        return lax.rem(gx + da + 4, 4) * 32 + lax.rem(col + db + 32, 32)

    sides = ((1, 0, 1, 0), (0, 1, -1, 0), (3, 2, 0, 1), (2, 3, 0, -1), (1, 4, 1, 1), (1, 5, 1, -1), (0, 6, -1, 1), (0, 7, -1, -1))
    borders = []
    for edge, slot, da, db in sides:
        borders.append(
            pltpu.make_async_remote_copy(
                src_ref=edges.at[edge],
                dst_ref=halo.at[slot],
                send_sem=ss.at[2],
                recv_sem=rh.at[slot],
                device_id=place_of(neighbour(da, db)),
                device_id_type=MESH,
            )
        )
    for copy in borders:
        copy.start()

    def ship(k, _):
        p = lax.rem(me + k, 128)
        group = k // U
        pltpu.make_async_remote_copy(
            src_ref=send.at[p], dst_ref=recv.at[me], send_sem=ss.at[0], recv_sem=ra.at[group],
            device_id=place_of(p), device_id_type=MESH).start()
        pltpu.make_async_remote_copy(
            src_ref=scell.at[p], dst_ref=rcell.at[me], send_sem=ss.at[1], recv_sem=rb.at[group],
            device_id=place_of(p), device_id_type=MESH).start()
        return _

    lax.fori_loop(1, 128, ship, 0)

    def bytes_of(n, src, dst, s_sem, r_sem):
        return pltpu.make_async_remote_copy(
            src_ref=src.at[pl.ds(0, n)], dst_ref=dst.at[pl.ds(0, n)], send_sem=s_sem, recv_sem=r_sem,
            device_id=place_of(lax.rem(me + 1, 128)), device_id_type=MESH)

    for copy in borders:
        copy.wait_recv()
    masks = [(gx > 0).astype(F32), (gx < 3).astype(F32), (col > 0).astype(F32), (col < 31).astype(F32)]
    setup(vel, halo, fh, fl, tab, masks)

    def group_of(i):
        for u in range(U):
            s = lax.rem(me - (i * U + u) + 128, 128)
            v = recv[s]
            cell = rcell[s]
            out[:, pl.ds(pl.multiple_of(s * 256, 256), 256)] = interp(v, cell, fh, fl, tab)
            cout[s] = cell.astype(I32)

    bytes_of(U - 1, send, recv, ss.at[0], ra.at[0]).wait_recv()
    bytes_of(U - 1, scell, rcell, ss.at[1], rb.at[0]).wait_recv()

    def step(i, _):
        group_of(i)

        @pl.when(i < 128 // U - 1)
        def _wait():
            bytes_of(U, send, recv, ss.at[0], ra.at[i + 1]).wait_recv()
            bytes_of(U, scell, rcell, ss.at[1], rb.at[i + 1]).wait_recv()

        return _

    lax.fori_loop(0, 128 // U, step, 0)
    bytes_of(127, send, recv, ss.at[0], ra.at[0]).wait_send()
    bytes_of(127, scell, rcell, ss.at[1], rb.at[0]).wait_send()
    bytes_of(8, halo, halo, ss.at[2], rh.at[0]).wait_send()


def vmem(n):
    return [pl.BlockSpec(memory_space=pltpu.VMEM)] * n


def shards(particles, dest_key, cell_a, cell_b, velocity):
    send, scell, edges = pl.pallas_call(
        bucket_edges,
        out_shape=(
            jax.ShapeDtypeStruct((128, 8, 256), F32),
            jax.ShapeDtypeStruct((128, 1, 256), F32),
            jax.ShapeDtypeStruct((4, 2, 256), F32),
        ),
        in_specs=vmem(5),
        out_specs=vmem(3),
        scratch_shapes=[
            pltpu.VMEM((32, 128, 256), BF),
            pltpu.VMEM((8, 8704), F32),
            pltpu.VMEM((8, 8704), F32),
            pltpu.VMEM((576, 256), F32),
            pltpu.VMEM((8, 128), I32),
            pltpu.SMEM((8, 128), I32),
            pltpu.SemaphoreType.DMA,
        ],
        name="bucket",
    )(velocity, particles, dest_key.reshape(64, 128), cell_a.reshape(64, 128), cell_b.reshape(64, 128))
    binned, cells = pl.pallas_call(
        exchange,
        out_shape=(jax.ShapeDtypeStruct((8, 32768), F32), jax.ShapeDtypeStruct((128, 1, 256), I32)),
        in_specs=vmem(4),
        out_specs=vmem(2),
        scratch_shapes=[
            pltpu.VMEM((128, 8, 256), F32),
            pltpu.VMEM((128, 1, 256), F32),
            pltpu.VMEM((8, 2, 256), F32),
            pltpu.VMEM((272, 256), BF),
            pltpu.VMEM((272, 256), BF),
            pltpu.VMEM((2, 8, 128), F32),
            pltpu.SemaphoreType.DMA((3,)),
            pltpu.SemaphoreType.DMA((128 // U,)),
            pltpu.SemaphoreType.DMA((128 // U,)),
            pltpu.SemaphoreType.DMA((8,)),
        ],
        compiler_params=pltpu.CompilerParams(collective_id=0, has_side_effects=True),
        name="exchange",
    )(velocity, edges, send, scell)
    return binned, cells.reshape(-1)


def solution(mesh):
    in_specs = (P(None, AXES), P(AXES), P(AXES), P(AXES), P(None, "gx", ("gy", "gz")))
    return jax.shard_map(
        shards, mesh=mesh, in_specs=in_specs, out_specs=(P(None, AXES), P(AXES)), check_vma=False
    )
```

time: 261 us -> 68.6 us (0.26)
  the two profiles are of different devices: /device:TPU:43 before, /device:TPU:33 now
where the time goes in v1:
time: 68.6 us; the launch traced here: 68.4 us
  Pallas kernels  64.8 us (94%)
  local copies, waits for them, and re-layouts  2.97 us (4%)
    pallas_call x1, Pallas kernels, shards(): pl.pallas_call(exchange, out_shape=(jax.ShapeDtypeStruct((8, 32768), F32)...  49.9 us
    pallas_call x1, Pallas kernels, shards(): pl.pallas_call(bucket_edges, out_shape=(jax.ShapeDtypeStruct((128, 8, 256...  14.9 us
    unnamed x4, local copies, waits for them, and re-layouts  2.97 us

profile of v1, /device:TPU:33, one launch (start us, length us, event | category | flops | bytes accessed | tf_op | source)
XLA Modules:
  0.0 68.4 jit_solution(6327227254021029760)
XLA Ops:
  0.6 14.9 %bucket.1 = (f32[128,8,256]{2,1,0:T(8,128)}, f32[128,1,256]{2,1,0:T(1,128)}, f32[4,2,256]{2,1,0:T(2,128)}) custom-call(f32[2,256,128]{2,1,0:T(8,128)} %vel.3, f32[8,8192]{1,0:T(8,128)} %part.1, s32[64,128]{1,0:T(8,128)} %bitcast.5, s32[64,128]{1,0:T(8,128)} %bitcast.6, s32[64,128]{1,0:T(8,128)} %bitcast.7), custom_call_target="tpu_custom_call" | custom-call | tf_op jit(solution)/shard_map/bucket/pallas_call | solution.py:284
  15.5 49.9 %exchange.1 = (f32[8,32768]{1,0:T(8,128)}, s32[128,1,256]{2,1,0:T(1,128)}) custom-call(f32[2,256,128]{2,1,0:T(8,128)} %vel.3, f32[4,2,256]{2,1,0:T(2,128)} %get-tuple-element.7.edges, f32[128,8,256]{2,1,0:T(8,128)} %get-tuple-element.8.send, f32[128,1,256]{2,1,0:T(1,128)} %get-tuple-element.9.scell), custom_call_target="tpu_custom_call" | custom-call | tf_op jit(solution)/shard_map/exchange/pallas_call | solution.py:304
  65.4 0.0 copy-start
  65.4 2.3 %copy.9 = f32[8,32768]{1,0:T(8,128)} copy(f32[8,32768]{1,0:T(8,128)} %get-tuple-element.14) | data formatting | bytes 2097152
  67.7 0.0 copy-done
  67.7 0.7 copy.10
Async XLA Ops:
  65.4 2.3 %copy-start = (s32[128,1,256]{2,1,0:T(1,128)S(1)}, s32[128,1,256]{2,1,0:T(1,128)}, u32[]{:S(2)}) copy-start(s32[128,1,256]{2,1,0:T(1,128)} %get-tuple-element.11) | copy-start | bytes 393220

commit v2 on v1

v2 whole, which is shorter than its diff:
```python
import jax
import jax.numpy as jnp
from jax import lax
from jax.experimental import pallas as pl
from jax.experimental.pallas import tpu as pltpu
from jax.sharding import PartitionSpec as P

BF = jnp.bfloat16
F32 = jnp.float32
I32 = jnp.int32
NT = (((1,), (1,)), ((), ()))
AXES = ("gx", "gy", "gz")
LOGICAL = pl.DeviceIdType.LOGICAL
SIDES = ((1, 1, 0), (0, -1, 0), (3, 0, 1), (2, 0, -1), (1, 1, 1), (1, 1, -1), (0, -1, 1), (0, -1, -1))


def dotf(a, b):
    return jnp.dot(a, b, preferred_element_type=F32)


PB=8
UB=8
XB=16
U=16

def row256(ref, j):
    r = ref[pl.ds(2*j,2),:]
    return jnp.concatenate([r[0:1],r[1:2]],axis=1)

def bucket(part, dest, ca, cb, out, oh, pos_s, srt, csrt, acc, stv, sts, sem, first):
    nb=32
    one=jnp.ones((),BF); zero=jnp.zeros((),BF)
    iod=lax.broadcasted_iota(I32,(128,256),0).astype(F32).astype(BF)
    def onehot(j,S):
        d=row256(dest,j).astype(F32).astype(BF)
        o=jnp.where(iod==jnp.broadcast_to(d,(128,256)),one,zero)
        oh[j]=o
        return S+o
    S=lax.fori_loop(0,nb,onehot,jnp.zeros((128,256),BF),unroll=4)
    ones=jnp.ones((256,256),BF)
    tot=dotf(S,ones)
    low=(lax.broadcasted_iota(I32,(128,128),0)>lax.broadcasted_iota(I32,(128,128),1)).astype(F32).astype(BF)
    start=dotf(low,tot.astype(BF))
    diag=lax.broadcasted_iota(I32,(128,128),0)==lax.broadcasted_iota(I32,(128,128),1)
    srow=jnp.sum(jnp.where(diag,start[:,:128],0.),axis=0,keepdims=True)
    trow=jnp.sum(jnp.where(diag,tot[:,:128],0.),axis=0,keepdims=True)
    tile=jnp.floor(srow*(1/128))
    sh=srow-128.*tile
    stv[0:1,:]=tile.astype(I32)
    stv[1:2,:]=jnp.where(sh==0.,0.,128.-sh).astype(I32)
    stv[2:3,:]=(128.-sh).astype(I32)
    stv[3:4,:]=trow.astype(I32)
    cp=pltpu.make_async_copy(stv,sts,sem)
    cp.start()
    up=(lax.broadcasted_iota(I32,(256,256),0)<lax.broadcasted_iota(I32,(256,256),1)).astype(F32).astype(BF)
    upones=jnp.concatenate([up,ones],axis=0)
    lane=lax.broadcasted_iota(I32,(128,256),1).astype(F32)
    C0=jnp.floor((start+255.-lane)*(1/256)).astype(BF)
    def ranks(jj,C):
        for u in range(PB):
            j=jj*PB+u
            o=oh[j]
            x=dotf(jnp.concatenate([o,C],axis=1),upones)
            pos=jnp.sum(o.astype(F32)*x,axis=0,keepdims=True)
            hi=jnp.floor(pos*(1/256))
            pos_s[j,0:1,:]=hi
            pos_s[j,1:2,:]=pos-256.*hi
            C=C+o
        return C
    lax.fori_loop(0,nb//PB,ranks,C0)
    acc[...]=jnp.zeros_like(acc)
    iol=lax.broadcasted_iota(I32,(256,256),0).astype(F32).astype(BF)
    s16=lax.broadcasted_iota(I32,(16,256),0)
    half=(s16//8).astype(F32).astype(BF)
    i32_=lax.broadcasted_iota(I32,(32,256),0).astype(F32).astype(BF)
    def place(jj,_):
        As=[];Ls=[]
        for u in range(UB):
            j=jj*UB+u
            hi=pos_s[j,0:1,:].astype(BF); lo=pos_s[j,1:2,:].astype(BF)
            lot=jnp.where(iol==jnp.broadcast_to(lo,(256,256)),one,zero)
            v=part[:,pl.ds(pl.multiple_of(j*256,256),256)]
            vh=v.astype(BF).astype(F32); vl=v-vh
            vh2=jnp.concatenate([vh,vh],axis=0).astype(BF)
            vl2=jnp.concatenate([vl,vl],axis=0).astype(BF)
            h16=jnp.broadcast_to(hi,(16,256))-half
            hs=[];ls=[]
            for k in range(16):
                m=h16==float(2*k)
                hs.append(jnp.where(m,vh2,zero)); ls.append(jnp.where(m,vl2,zero))
            m32=i32_==jnp.broadcast_to(hi,(32,256))
            a=row256(ca,j).astype(F32).astype(BF); b=row256(cb,j).astype(F32).astype(BF)
            As.append(jnp.concatenate(hs+ls+[jnp.where(m32,jnp.broadcast_to(a,(32,256)),zero),jnp.where(m32,jnp.broadcast_to(b,(32,256)),zero)],axis=0))
            Ls.append(lot)
        acc[...]+=lax.dot_general(jnp.concatenate(As,axis=1),jnp.concatenate(Ls,axis=1),NT,preferred_element_type=F32)
        return _
    lax.fori_loop(0,nb//UB,place,0)
    for h in range(32):
        x=acc[h*8:(h+1)*8]+acc[256+h*8:256+(h+1)*8]
        srt[2*h]=x[:,:128]; srt[2*h+1]=x[:,128:]
    cc=acc[512:544]*128.+acc[544:576]
    for t in range(64):
        r=cc[t//2:t//2+1,(t%2)*128:(t%2)*128+128]
        for i in range(3):
            if t-i>=0: csrt[t-i,i:i+1,:]=r
    cp.wait()
    lane=lax.broadcasted_iota(I32,(8,128),1)
    sub=lax.broadcasted_iota(I32,(8,128),0)
    place256=lane+128*sub
    def expand(dd,_):
        e=first+dd
        e=jnp.where(e>=128//XB,e-128//XB,e)
        for u in range(XB):
            d=e*XB+u
            t=jnp.clip(sts[0,d],0,64); rot=sts[1,d]; thr=sts[2,d]; n=sts[3,d]
            rs=[pltpu.roll(srt[t+i],rot,1) for i in range(3)]
            c=pltpu.roll(csrt[t],rot,1)
            keep=lane<thr
            for i in range(2):
                out[d,i]=jnp.where(lane<n-128*i,jnp.where(keep,rs[i],rs[i+1]),0.)
            out[d,2]=jnp.where(place256<n,jnp.where(keep,c,pltpu.roll(c,7,0)),-1.)
        return _
    lax.fori_loop(0,128//XB,expand,0)

def split(x):
    h=x.astype(BF); return h,(x-h.astype(F32)).astype(BF)
def weights(t):
    return 0.5*t*(t-1.), 1.-t*t, 0.5*t*(t+1.)
def setup(vel, halo, fh, fl, tab, masks):
    mu,md,ml,mr=masks
    lane=lax.broadcasted_iota(I32,(1,128),1)
    z8=jnp.zeros((8,256),F32)
    for c in range(2):
        ft=jnp.transpose(vel[c])
        lrow=halo[2][c:c+1,:]*ml
        rrow=halo[3][c:c+1,:]*mr
        e=jnp.concatenate([lrow,ft,rrow,jnp.zeros((6,256),F32)],axis=0)
        h,l=split(e)
        fh[c*136:(c+1)*136]=h; fl[c*136:(c+1)*136]=l
        rows=[]
        for (mid,lc,rc,m) in ((0,4,5,mu),(1,6,7,md)):
            r=halo[mid][c:c+1,:128]*m
            le=halo[lc][c:c+1,:128]*(m*ml); re=halo[rc][c:c+1,:128]*(m*mr)
            rows.append(jnp.where(lane==0,pltpu.roll(le,1,1),pltpu.roll(r,1,1)))
            rows.append(r)
            rows.append(jnp.where(lane==127,pltpu.roll(re,127,1),pltpu.roll(r,127,1)))
        tab[c]=jnp.concatenate(rows+[jnp.zeros((2,128),F32)],axis=0)
def cellparts(cell):
    cm=jnp.maximum(cell,0.)
    a=jnp.floor(cm*(1/128)); b=cm-128.*a
    return a,b
def pick(rows, bits):
    level=list(rows)
    for m in bits:
        level=[jnp.where(m,level[2*k+1],level[2*k]) for k in range(len(level)//2)]
    return level[0]
def interp(v, cell, fh, fl, tab):
    n=v.shape[1]
    zero=jnp.zeros((),BF)
    f=v[0:1]; g=v[1:2]
    live=cell>=0.
    a,b=cellparts(cell)
    wf=weights(f); wg=weights(g)
    ga=jnp.floor((a-1.)*(1/16)); oa=(a-1.)-16.*ga
    gab=jnp.broadcast_to(ga.astype(BF),(16,n))
    d=lax.broadcasted_iota(I32,(16,n),0).astype(F32).astype(BF)-jnp.broadcast_to(oa.astype(BF),(16,n))
    hl=[split(w) for w in wf]
    m0=d==0;m1=d==1;m2=d==2;q1=d==-15;q2=d==-14
    pats=[]
    for i in range(2):
        w=[jnp.broadcast_to(x[i],(16,n)) for x in hl]
        pats.append((jnp.where(m0,w[0],jnp.where(m1,w[1],jnp.where(m2,w[2],zero))),
                     jnp.where(q1,w[1],jnp.where(q2,w[2],zero))))
    ms=[gab==float(G) for G in range(-1,16)]
    W=[jnp.concatenate([jnp.where(ms[G+1],pa,jnp.where(ms[G],pb,zero)) for G in range(16)],axis=0) for pa,pb in pats]
    H=fh[...]; L=fl[...]
    R=dotf(H,W[0])+dotf(L,W[0])+dotf(H,W[1])
    gb=jnp.floor(b*(1/8)); ob=b-8.*gb
    s8=lax.broadcasted_iota(I32,(8,n),0).astype(F32)
    d8=s8-ob
    pa=jnp.where(d8==0,wg[0],jnp.where(d8==1,wg[1],jnp.where(d8==2,wg[2],0.)))
    pb=jnp.where(d8==-7,wg[1],jnp.where(d8==-6,wg[2],0.))
    gi=jnp.broadcast_to(gb,(8,n)).astype(I32)
    bits=[(gi&(1<<k))!=0 for k in range(4)]
    accs=[]
    for c in range(2):
        rows=[R[c*136+8*G:c*136+8*G+8] for G in range(17)]
        accs.append((pick(rows[:16],bits),pick(rows[1:],bits)))
    si=lax.broadcasted_iota(I32,(8,n),0)
    wj=jnp.where((si==0)|(si==3),wg[0],jnp.where((si==1)|(si==4),wg[1],wg[2]))
    up=jnp.where(a==0.,wf[0],0.); dn=jnp.where(a==255.,wf[2],0.)
    Pm=jnp.where(si<3,up,jnp.where(si<6,dn,0.))*wj
    bi=jnp.broadcast_to(b.astype(I32),(8,n))
    out=v
    for c in range(2):
        T=tab[c]
        corr=jnp.concatenate([jnp.take_along_axis(T,bi[:,128*i:128*(i+1)],axis=1) for i in range(n//128)],axis=1)
        sp=jnp.sum(pa*accs[c][0]+pb*accs[c][1]+Pm*corr,axis=0,keepdims=True)
        disp=jnp.where(live,0.5*sp,0.)
        out=out+jnp.where(si==2+c,disp,0.)
    return out


def fused(vel, part, dest, ca, cb, out, cout, send, recv, edges, halo, fh, fl, tab, oh, pos_s, srt, csrt, acc, stv, sts, sem, ss, ra, rh):
    gx = lax.axis_index("gx")
    col = lax.axis_index("gy") * 2 + lax.axis_index("gz")
    me = gx * 32 + col
    barrier = pltpu.get_barrier_semaphore()

    def other(k):
        p = me + k
        return jnp.where(p >= 128, p - 128, p)

    def greet(k, _):
        pl.semaphore_signal(barrier, inc=1, device_id=other(k), device_id_type=LOGICAL)
        return _

    lax.fori_loop(1, 128, greet, 0)
    for c in range(2):
        zeros = jnp.zeros((1, 128), F32)
        edges[0, c : c + 1, :] = jnp.concatenate([vel[c, 0:1, :], zeros], axis=1)
        edges[1, c : c + 1, :] = jnp.concatenate([vel[c, 255:256, :], zeros], axis=1)
        turned = jnp.transpose(vel[c])
        edges[2, c : c + 1, :] = turned[0:1]
        edges[3, c : c + 1, :] = turned[127:128]
    bucket(part, dest, ca, cb, send, oh, pos_s, srt, csrt, acc, stv, sts, sem, me // XB)
    recv[me] = send[me]
    pl.semaphore_wait(barrier, 127)

    def neighbour(da, db):
        return lax.rem(gx + da + 4, 4) * 32 + lax.rem(col + db + 32, 32)

    borders = []
    for slot, (edge, da, db) in enumerate(SIDES):
        borders.append(
            pltpu.make_async_remote_copy(
                src_ref=edges.at[edge],
                dst_ref=halo.at[slot],
                send_sem=ss.at[1],
                recv_sem=rh.at[slot],
                device_id=neighbour(da, db),
                device_id_type=LOGICAL,
            )
        )
    for copy in borders:
        copy.start()

    for group in range(128 // U):

        def ship(k, _):
            p = other(k)
            pltpu.make_async_remote_copy(
                src_ref=send.at[p],
                dst_ref=recv.at[me],
                send_sem=ss.at[0],
                recv_sem=ra.at[group],
                device_id=p,
                device_id_type=LOGICAL,
            ).start()
            return _

        lax.fori_loop(max(1, group * U), group * U + U, ship, 0)

    def bytes_of(n, r_sem):
        return pltpu.make_async_remote_copy(
            src_ref=send.at[pl.ds(0, n)],
            dst_ref=recv.at[pl.ds(0, n)],
            send_sem=ss.at[0],
            recv_sem=r_sem,
            device_id=other(1),
            device_id_type=LOGICAL,
        )

    for copy in borders:
        copy.wait_recv()
    masks = [(gx > 0).astype(F32), (gx < 3).astype(F32), (col > 0).astype(F32), (col < 31).astype(F32)]
    setup(vel, halo, fh, fl, tab, masks)
    bytes_of(U - 1, ra.at[0]).wait_recv()

    def step(i, _):
        for u in range(U):
            s = me - (i * U + u)
            s = jnp.where(s < 0, s + 128, s)
            block = recv[s]
            v = jnp.concatenate([block[0], block[1]], axis=1)
            cell = jnp.concatenate([block[2, 0:1], block[2, 1:2]], axis=1)
            out[:, pl.ds(pl.multiple_of(s * 256, 256), 256)] = interp(v, cell, fh, fl, tab)
            cout[s] = cell.astype(I32)

        @pl.when(i < 128 // U - 1)
        def _wait():
            bytes_of(U, ra.at[i + 1]).wait_recv()

        return _

    lax.fori_loop(0, 128 // U, step, 0)
    bytes_of(127, ra.at[0]).wait_send()
    pltpu.make_async_remote_copy(
        src_ref=halo, dst_ref=halo, send_sem=ss.at[1], recv_sem=rh.at[0], device_id=other(1), device_id_type=LOGICAL
    ).wait_send()


def shards(particles, dest_key, cell_a, cell_b, velocity):
    vmem = pl.BlockSpec(memory_space=pltpu.VMEM)
    binned, cells = pl.pallas_call(
        fused,
        out_shape=(jax.ShapeDtypeStruct((8, 32768), F32), jax.ShapeDtypeStruct((128, 1, 256), I32)),
        in_specs=[vmem] * 5,
        out_specs=[vmem] * 2,
        scratch_shapes=[
            pltpu.VMEM((128, 3, 8, 128), F32),
            pltpu.VMEM((128, 3, 8, 128), F32),
            pltpu.VMEM((4, 2, 256), F32),
            pltpu.VMEM((8, 2, 256), F32),
            pltpu.VMEM((272, 256), BF),
            pltpu.VMEM((272, 256), BF),
            pltpu.VMEM((2, 8, 128), F32),
            pltpu.VMEM((32, 128, 256), BF),
            pltpu.VMEM((32, 2, 256), F32),
            pltpu.VMEM((67, 8, 128), F32),
            pltpu.VMEM((67, 8, 128), F32),
            pltpu.VMEM((576, 256), F32),
            pltpu.VMEM((8, 128), I32),
            pltpu.SMEM((8, 128), I32),
            pltpu.SemaphoreType.DMA,
            pltpu.SemaphoreType.DMA((2,)),
            pltpu.SemaphoreType.DMA((128 // U,)),
            pltpu.SemaphoreType.DMA((8,)),
        ],
        compiler_params=pltpu.CompilerParams(collective_id=0, has_side_effects=True),
        name="rebin",
    )(velocity, particles, dest_key.reshape(64, 128), cell_a.reshape(64, 128), cell_b.reshape(64, 128))
    return binned, cells.reshape(-1)


def solution(mesh):
    in_specs = (P(None, AXES), P(AXES), P(AXES), P(AXES), P(None, "gx", ("gy", "gz")))
    return jax.shard_map(
        shards, mesh=mesh, in_specs=in_specs, out_specs=(P(None, AXES), P(AXES)), check_vma=False
    )
```

time: 68.6 us -> 59.6 us (0.87)
  the two profiles are of different devices: /device:TPU:33 before, /device:TPU:1 now
where the time goes in v2:
time: 59.6 us; the launch traced here: 59.5 us
  Pallas kernels  55.9 us (94%)
  local copies, waits for them, and re-layouts  2.97 us (5%)
  between operations  0.65 us (1%)
    pallas_call x1, Pallas kernels, shards(): pl.pallas_call(fused, out_shape=(jax.ShapeDtypeStruct((8, 32768), F32), j...  55.9 us
    unnamed x4, local copies, waits for them, and re-layouts  2.97 us

profile of v2, /device:TPU:1, one launch (start us, length us, event | category | flops | bytes accessed | tf_op | source)
XLA Modules:
  0.0 59.5 jit_solution(9417284132423056948)
XLA Ops:
  0.6 55.9 %rebin.1 = (f32[8,32768]{1,0:T(8,128)}, s32[128,1,256]{2,1,0:T(1,128)}) custom-call(f32[2,256,128]{2,1,0:T(8,128)} %vel.1, f32[8,8192]{1,0:T(8,128)} %part.1, s32[64,128]{1,0:T(8,128)} %bitcast.5, s32[64,128]{1,0:T(8,128)} %bitcast.6, s32[64,128]{1,0:T(8,128)} %bitcast.7), custom_call_target="tpu_custom_call" | custom-call | tf_op jit(solution)/shard_map/rebin/pallas_call | solution.py:305
  56.5 0.0 copy-start
  56.5 2.3 %copy.9 = f32[8,32768]{1,0:T(8,128)} copy(f32[8,32768]{1,0:T(8,128)} %get-tuple-element.8) | data formatting | bytes 2097152
  58.8 0.0 copy-done
  58.8 0.7 %copy.10 = s32[32768]{0:T(1024)} copy(s32[32768]{0:T(1024)S(1)} %bitcast.4) | data formatting | bytes 262144
Async XLA Ops:
  56.5 2.3 %copy-start = (s32[128,1,256]{2,1,0:T(1,128)S(1)}, s32[128,1,256]{2,1,0:T(1,128)}, u32[]{:S(2)}) copy-start(s32[128,1,256]{2,1,0:T(1,128)} %get-tuple-element.5) | copy-start | bytes 393220

commit v3 on v2

--- a/solution.py
+++ b/solution.py
@@ -22,12 +22,13 @@
 UB=8
 XB=16
 U=16
+STRIDE=27
 
 def row256(ref, j):
     r = ref[pl.ds(2*j,2),:]
     return jnp.concatenate([r[0:1],r[1:2]],axis=1)
 
-def bucket(part, dest, ca, cb, out, oh, pos_s, srt, csrt, acc, stv, sts, sem, first):
+def bucket(part, dest, ca, cb, out, cells, oh, pos_s, srt, csrt, acc, stv, sts, sem, target, turn, ship, ready, open_links):
     nb=32
     one=jnp.ones((),BF); zero=jnp.zeros((),BF)
     iod=lax.broadcasted_iota(I32,(128,256),0).astype(F32).astype(BF)
@@ -69,6 +70,7 @@
         return C
     lax.fori_loop(0,nb//PB,ranks,C0)
     acc[...]=jnp.zeros_like(acc)
+    ready()
     iol=lax.broadcasted_iota(I32,(256,256),0).astype(F32).astype(BF)
     s16=lax.broadcasted_iota(I32,(16,256),0)
     half=(s16//8).astype(F32).astype(BF)
@@ -105,22 +107,32 @@
             if t-i>=0: csrt[t-i,i:i+1,:]=r
     cp.wait()
     lane=lax.broadcasted_iota(I32,(8,128),1)
-    sub=lax.broadcasted_iota(I32,(8,128),0)
-    place256=lane+128*sub
-    def expand(dd,_):
-        e=first+dd
-        e=jnp.where(e>=128//XB,e-128//XB,e)
+    def expand(k):
+        d=target(k)
+        t=jnp.clip(sts[0,d],0,64); rot=sts[1,d]; thr=sts[2,d]; n=sts[3,d]
+        rs=[pltpu.roll(srt[t+i],rot,1) for i in range(3)]
+        c=pltpu.roll(csrt[t],rot,1)
+        keep=lane<thr
+        c1=jnp.where(keep[0:2],c[0:2],c[1:3])
+        for i in range(2):
+            live=lane<n-128*i
+            out[d,:,128*i:128*(i+1)]=jnp.where(live,jnp.where(keep,rs[i],rs[i+1]),0.)
+            cells[d,:,128*i:128*(i+1)]=jnp.where(live[0:1],c1[i:i+1],-1.)
+    def back(k):
+        k=k-STRIDE*XB%128
+        return jnp.where(k<0,k+128,k)
+    def deliver(i,k):
+        old=k
         for u in range(XB):
-            d=e*XB+u
-            t=jnp.clip(sts[0,d],0,64); rot=sts[1,d]; thr=sts[2,d]; n=sts[3,d]
-            rs=[pltpu.roll(srt[t+i],rot,1) for i in range(3)]
-            c=pltpu.roll(csrt[t],rot,1)
-            keep=lane<thr
-            for i in range(2):
-                out[d,i]=jnp.where(lane<n-128*i,jnp.where(keep,rs[i],rs[i+1]),0.)
-            out[d,2]=jnp.where(place256<n,jnp.where(keep,c,pltpu.roll(c,7,0)),-1.)
-        return _
-    lax.fori_loop(0,128//XB,expand,0)
+            k=turn(k)
+            expand(k)
+        @pl.when(i>0)
+        def _():
+            ship(i-1,back(old),XB)
+        return k
+    open_links()
+    k=lax.fori_loop(0,128//XB,deliver,0)
+    ship(128//XB-1,back(k),XB-1)
 
 def split(x):
     h=x.astype(BF); return h,(x-h.astype(F32)).astype(BF)
@@ -201,21 +213,35 @@
     return out
 
 
-def fused(vel, part, dest, ca, cb, out, cout, send, recv, edges, halo, fh, fl, tab, oh, pos_s, srt, csrt, acc, stv, sts, sem, ss, ra, rh):
+def fused(vel_in, part_in, dest_in, ca_in, cb_in, out, cout, vel, part, dest, ca, cb, send, scell, recv, rcell, edges, halo,
+          fh, fl, tab, oh, pos_s, srt, csrt, acc, stv, sts, sem, ins, ss, ra, rb, rh):
+    loads = [
+        pltpu.make_async_copy(src, dst, ins.at[i])
+        for i, (src, dst) in enumerate(((dest_in, dest), (vel_in, vel), (ca_in, ca), (cb_in, cb), (part_in, part)))
+    ]
+    for load in loads:
+        load.start()
     gx = lax.axis_index("gx")
     col = lax.axis_index("gy") * 2 + lax.axis_index("gz")
     me = gx * 32 + col
     barrier = pltpu.get_barrier_semaphore()
 
+    def wrap(p):
+        return jnp.where(p >= 128, p - 128, p)
+
     def other(k):
-        p = me + k
-        return jnp.where(p >= 128, p - 128, p)
+        return wrap(me + k)
+
+    def turn(k):
+        return wrap(k + STRIDE)
 
     def greet(k, _):
         pl.semaphore_signal(barrier, inc=1, device_id=other(k), device_id_type=LOGICAL)
         return _
 
     lax.fori_loop(1, 128, greet, 0)
+    loads[0].wait()
+    loads[1].wait()
     for c in range(2):
         zeros = jnp.zeros((1, 128), F32)
         edges[0, c : c + 1, :] = jnp.concatenate([vel[c, 0:1, :], zeros], axis=1)
@@ -223,9 +249,6 @@
         turned = jnp.transpose(vel[c])
         edges[2, c : c + 1, :] = turned[0:1]
         edges[3, c : c + 1, :] = turned[127:128]
-    bucket(part, dest, ca, cb, send, oh, pos_s, srt, csrt, acc, stv, sts, sem, me // XB)
-    recv[me] = send[me]
-    pl.semaphore_wait(barrier, 127)
 
     def neighbour(da, db):
         return lax.rem(gx + da + 4, 4) * 32 + lax.rem(col + db + 32, 32)
@@ -236,68 +259,82 @@
             pltpu.make_async_remote_copy(
                 src_ref=edges.at[edge],
                 dst_ref=halo.at[slot],
-                send_sem=ss.at[1],
+                send_sem=ss.at[2],
                 recv_sem=rh.at[slot],
                 device_id=neighbour(da, db),
                 device_id_type=LOGICAL,
             )
         )
-    for copy in borders:
-        copy.start()
-
-    for group in range(128 // U):
-
-        def ship(k, _):
+
+    def ready():
+        for load in loads[2:]:
+            load.wait()
+
+    def ship(group, k, count):
+        for u in range(count):
+            k = turn(k)
             p = other(k)
-            pltpu.make_async_remote_copy(
-                src_ref=send.at[p],
-                dst_ref=recv.at[me],
-                send_sem=ss.at[0],
-                recv_sem=ra.at[group],
-                device_id=p,
-                device_id_type=LOGICAL,
-            ).start()
-            return _
-
-        lax.fori_loop(max(1, group * U), group * U + U, ship, 0)
-
-    def bytes_of(n, r_sem):
+            for src, dst, lane_sem, done in ((send, recv, ss.at[0], ra), (scell, rcell, ss.at[1], rb)):
+                pltpu.make_async_remote_copy(
+                    src_ref=src.at[p],
+                    dst_ref=dst.at[me],
+                    send_sem=lane_sem,
+                    recv_sem=done.at[group],
+                    device_id=p,
+                    device_id_type=LOGICAL,
+                ).start()
+
+    def open_links():
+        pl.semaphore_wait(barrier, 127)
+        for copy in borders:
+            copy.start()
+
+    bucket(part, dest, ca, cb, send, scell, oh, pos_s, srt, csrt, acc, stv, sts, sem, other, turn, ship, ready, open_links)
+    recv[me] = send[me]
+    rcell[me] = scell[me]
+
+    def bytes_of(n, src, dst, s_sem, r_sem):
         return pltpu.make_async_remote_copy(
-            src_ref=send.at[pl.ds(0, n)],
-            dst_ref=recv.at[pl.ds(0, n)],
-            send_sem=ss.at[0],
+            src_ref=src.at[pl.ds(0, n)],
+            dst_ref=dst.at[pl.ds(0, n)],
+            send_sem=s_sem,
             recv_sem=r_sem,
             device_id=other(1),
             device_id_type=LOGICAL,
         )
 
+    def arrived(group, n):
+        bytes_of(n, send, recv, ss.at[0], ra.at[group]).wait_recv()
+        bytes_of(n, scell, rcell, ss.at[1], rb.at[group]).wait_recv()
+
     for copy in borders:
         copy.wait_recv()
     masks = [(gx > 0).astype(F32), (gx < 3).astype(F32), (col > 0).astype(F32), (col < 31).astype(F32)]
     setup(vel, halo, fh, fl, tab, masks)
-    bytes_of(U - 1, ra.at[0]).wait_recv()
-
-    def step(i, _):
+    last = 128 // U - 1
+
+    def step(i, k):
+        @pl.when(i < last)
+        def _full():
+            arrived(i, U)
+
+        @pl.when(i == last)
+        def _short():
+            arrived(last, U - 1)
+
         for u in range(U):
-            s = me - (i * U + u)
+            k = turn(k)
+            s = me - k
             s = jnp.where(s < 0, s + 128, s)
-            block = recv[s]
-            v = jnp.concatenate([block[0], block[1]], axis=1)
-            cell = jnp.concatenate([block[2, 0:1], block[2, 1:2]], axis=1)
-            out[:, pl.ds(pl.multiple_of(s * 256, 256), 256)] = interp(v, cell, fh, fl, tab)
+            cell = rcell[s]
+            out[:, pl.ds(pl.multiple_of(s * 256, 256), 256)] = interp(recv[s], cell, fh, fl, tab)
             cout[s] = cell.astype(I32)
-
-        @pl.when(i < 128 // U - 1)
-        def _wait():
-            bytes_of(U, ra.at[i + 1]).wait_recv()
-
-        return _
+        return k
 
     lax.fori_loop(0, 128 // U, step, 0)
-    bytes_of(127, ra.at[0]).wait_send()
-    pltpu.make_async_remote_copy(
-        src_ref=halo, dst_ref=halo, send_sem=ss.at[1], recv_sem=rh.at[0], device_id=other(1), device_id_type=LOGICAL
-    ).wait_send()
+    bytes_of(127, send, recv, ss.at[0], ra.at[0]).wait_send()
+    bytes_of(127, scell, rcell, ss.at[1], rb.at[0]).wait_send()
+    bytes_of(8, halo, halo, ss.at[2], rh.at[0]).wait_send()
 
 
 def shards(particles, dest_key, cell_a, cell_b, velocity):
@@ -305,11 +342,18 @@
     binned, cells = pl.pallas_call(
         fused,
         out_shape=(jax.ShapeDtypeStruct((8, 32768), F32), jax.ShapeDtypeStruct((128, 1, 256), I32)),
-        in_specs=[vmem] * 5,
+        in_specs=[pl.BlockSpec(memory_space=pl.ANY)] * 5,
         out_specs=[vmem] * 2,
         scratch_shapes=[
-            pltpu.VMEM((128, 3, 8, 128), F32),
-            pltpu.VMEM((128, 3, 8, 128), F32),
+            pltpu.VMEM((2, 256, 128), F32),
+            pltpu.VMEM((8, 8192), F32),
+            pltpu.VMEM((64, 128), I32),
+            pltpu.VMEM((64, 128), I32),
+            pltpu.VMEM((64, 128), I32),
+            pltpu.VMEM((128, 8, 256), F32),
+            pltpu.VMEM((128, 1, 256), F32),
+            pltpu.VMEM((128, 8, 256), F32),
+            pltpu.VMEM((128, 1, 256), F32),
             pltpu.VMEM((4, 2, 256), F32),
             pltpu.VMEM((8, 2, 256), F32),
             pltpu.VMEM((272, 256), BF),
@@ -323,7 +367,9 @@
             pltpu.VMEM((8, 128), I32),
             pltpu.SMEM((8, 128), I32),
             pltpu.SemaphoreType.DMA,
-            pltpu.SemaphoreType.DMA((2,)),
+            pltpu.SemaphoreType.DMA((5,)),
+            pltpu.SemaphoreType.DMA((3,)),
+            pltpu.SemaphoreType.DMA((128 // U,)),
             pltpu.SemaphoreType.DMA((128 // U,)),
             pltpu.SemaphoreType.DMA((8,)),
         ],

time: 59.6 us -> 41.7 us (0.70)
  Pallas kernels: 55.9 us -> 37.9 us
    pallas_call x1, Pallas kernels: 55.9 us -> 37.9 us  [shards(): pl.pallas_call(fused, out_shape=(jax.ShapeDtypeStruct((8, 32768), F32), j...]
where the time goes in v3:
time: 41.7 us; the launch traced here: 41.6 us
  Pallas kernels  37.9 us (91%)
  local copies, waits for them, and re-layouts  2.97 us (7%)
  between operations  0.65 us (2%)
    pallas_call x1, Pallas kernels, shards(): pl.pallas_call(fused, out_shape=(jax.ShapeDtypeStruct((8, 32768), F32), j...  37.9 us
    unnamed x4, local copies, waits for them, and re-layouts  2.97 us

profile of v3, /device:TPU:1, one launch (start us, length us, event | category | flops | bytes accessed | tf_op | source)
XLA Modules:
  0.0 41.6 jit_solution(10362893388872995518)
XLA Ops:
  0.6 37.9 %rebin.1 = (f32[8,32768]{1,0:T(8,128)}, s32[128,1,256]{2,1,0:T(1,128)}) custom-call(f32[2,256,128]{2,1,0:T(8,128)} %vel_in.1, f32[8,8192]{1,0:T(8,128)} %part_in.1, s32[64,128]{1,0:T(8,128)} %bitcast.5, s32[64,128]{1,0:T(8,128)} %bitcast.6, s32[64,128]{1,0:T(8,128)} %bitcast.7), custom_call_target="tpu_custom_call" | custom-call | tf_op jit(solution)/shard_map/rebin/pallas_call | solution.py:342
  38.6 0.0 copy-start
  38.6 2.3 %copy.9 = f32[8,32768]{1,0:T(8,128)} copy(f32[8,32768]{1,0:T(8,128)} %get-tuple-element.8) | data formatting | bytes 2097152
  40.9 0.0 copy-done
  40.9 0.7 %copy.10 = s32[32768]{0:T(1024)} copy(s32[32768]{0:T(1024)S(1)} %bitcast.4) | data formatting | bytes 262144
Async XLA Ops:
  38.6 2.3 %copy-start = (s32[128,1,256]{2,1,0:T(1,128)S(1)}, s32[128,1,256]{2,1,0:T(1,128)}, u32[]{:S(2)}) copy-start(s32[128,1,256]{2,1,0:T(1,128)} %get-tuple-element.5) | copy-start | bytes 393220

commit v4 on v3

--- a/solution.py
+++ b/solution.py
@@ -18,8 +18,8 @@
     return jnp.dot(a, b, preferred_element_type=F32)
 
 
-PB=8
-UB=8
+PB=16
+UB=16
 XB=16
 U=16
 STRIDE=27
@@ -312,15 +312,18 @@
     masks = [(gx > 0).astype(F32), (gx < 3).astype(F32), (col > 0).astype(F32), (col < 31).astype(F32)]
     setup(vel, halo, fh, fl, tab, masks)
     last = 128 // U - 1
+    per = U // XB
 
     def step(i, k):
         @pl.when(i < last)
         def _full():
-            arrived(i, U)
+            for q in range(per):
+                arrived(i * per + q, XB)
 
         @pl.when(i == last)
         def _short():
-            arrived(last, U - 1)
+            for q in range(per):
+                arrived(last * per + q, XB - (q == per - 1))
 
         for u in range(U):
             k = turn(k)
@@ -337,11 +340,31 @@
     bytes_of(8, halo, halo, ss.at[2], rh.at[0]).wait_send()
 
 
+def put_out(a_ref, b_ref, out, cout, sems):
+    copies = [pltpu.make_async_copy(a_ref, out, sems.at[0]), pltpu.make_async_copy(b_ref, cout, sems.at[1])]
+    for copy in copies:
+        copy.start()
+    for copy in copies:
+        copy.wait()
+
+
+def settle(binned, cells):
+    binned, cells = pl.pallas_call(
+        put_out,
+        out_shape=(jax.ShapeDtypeStruct(binned.shape, F32), jax.ShapeDtypeStruct(cells.shape, I32)),
+        in_specs=[pl.BlockSpec(memory_space=pltpu.VMEM)] * 2,
+        out_specs=[pl.BlockSpec(memory_space=pl.ANY)] * 2,
+        scratch_shapes=[pltpu.SemaphoreType.DMA((2,))],
+        name="settle",
+    )(pltpu.with_memory_space_constraint(binned, pltpu.VMEM), pltpu.with_memory_space_constraint(cells, pltpu.VMEM))
+    return binned, cells.reshape(-1)
+
+
 def shards(particles, dest_key, cell_a, cell_b, velocity):
     vmem = pl.BlockSpec(memory_space=pltpu.VMEM)
     binned, cells = pl.pallas_call(
         fused,
-        out_shape=(jax.ShapeDtypeStruct((8, 32768), F32), jax.ShapeDtypeStruct((128, 1, 256), I32)),
+        out_shape=(pltpu.VMEM((8, 32768), F32), pltpu.VMEM((128, 1, 256), I32)),
         in_specs=[pl.BlockSpec(memory_space=pl.ANY)] * 5,
         out_specs=[vmem] * 2,
         scratch_shapes=[
@@ -369,14 +392,14 @@
             pltpu.SemaphoreType.DMA,
             pltpu.SemaphoreType.DMA((5,)),
             pltpu.SemaphoreType.DMA((3,)),
-            pltpu.SemaphoreType.DMA((128 // U,)),
-            pltpu.SemaphoreType.DMA((128 // U,)),
+            pltpu.SemaphoreType.DMA((128 // XB,)),
+            pltpu.SemaphoreType.DMA((128 // XB,)),
             pltpu.SemaphoreType.DMA((8,)),
         ],
         compiler_params=pltpu.CompilerParams(collective_id=0, has_side_effects=True),
         name="rebin",
     )(velocity, particles, dest_key.reshape(64, 128), cell_a.reshape(64, 128), cell_b.reshape(64, 128))
-    return binned, cells.reshape(-1)
+    return settle(binned, cells)
 
 
 def solution(mesh):

time: 41.7 us -> 37.9 us (0.909)
  local copies, waits for them, and re-layouts: 2.97 us -> 0 us
  Pallas kernels: 37.9 us -> 37.2 us
    unnamed x4 -> x0, local copies, waits for them, and re-layouts: 2.97 us -> none
    pallas_call x1 -> x2, Pallas kernels: 37.9 us -> 37.2 us  [the longest x1 36.1 us: shards(): pl.pallas_call(fused, out_shape=(pltpu.VMEM((8, 32768), F32), pltpu.VMEM(...]
where the time goes in v4:
time: 37.9 us; the launch traced here: 37.8 us
  Pallas kernels  37.2 us (98%)
  between operations  0.64 us (2%)
    pallas_call x1, Pallas kernels, shards(): pl.pallas_call(fused, out_shape=(pltpu.VMEM((8, 32768), F32), pltpu.VMEM(...  36.1 us
    pallas_call x1, Pallas kernels, settle(): pl.pallas_call(put_out, out_shape=(jax.ShapeDtypeStruct(binned.shape, F32...  1.02 us

profile of v4, /device:TPU:1, one launch (start us, length us, event | category | flops | bytes accessed | tf_op | source)
XLA Modules:
  0.0 37.8 jit_solution(7659470106135369171)
XLA Ops:
  0.6 36.1 %rebin.1 = (f32[8,32768]{1,0:T(8,128)S(1)}, s32[128,1,256]{2,1,0:T(1,128)S(1)}) custom-call(f32[2,256,128]{2,1,0:T(8,128)} %vel_in.1, f32[8,8192]{1,0:T(8,128)} %part_in.1, s32[64,128]{1,0:T(8,128)} %bitcast.4, s32[64,128]{1,0:T(8,128)} %bitcast.5, s32[64,128]{1,0:T(8,128)} %bitcast.6), custom_call_target="tpu_custom_call" | custom-call | tf_op jit(solution)/shard_map/rebin/pallas_call | solution.py:365
  36.8 1.0 %settle.1 = (f32[8,32768]{1,0:T(8,128)}, s32[128,1,256]{2,1,0:T(1,128)}) custom-call(f32[8,32768]{1,0:T(8,128)S(1)} %get-tuple-element.6.a_ref, s32[128,1,256]{2,1,0:T(1,128)S(1)} %get-tuple-element.7.b_ref), custom_call_target="tpu_custom_call" | custom-call | tf_op jit(solution)/shard_map/settle/pallas_call | solution.py:352

commit v5 on v4

--- a/solution.py
+++ b/solution.py
@@ -20,15 +20,17 @@
 
 PB=16
 UB=16
-XB=16
 U=16
-STRIDE=27
+STEPS=((4,1),(2,2))
+SB=8
+TURN=tuple(27*u%128 for u in range(U))
+STEP=27*SB%128
 
 def row256(ref, j):
     r = ref[pl.ds(2*j,2),:]
     return jnp.concatenate([r[0:1],r[1:2]],axis=1)
 
-def bucket(part, dest, ca, cb, out, cells, oh, pos_s, srt, csrt, acc, stv, sts, sem, target, turn, ship, ready, open_links):
+def bucket(part, dest, ca, cb, out, cells, oh, pos_s, srt, csrt, acc, stv, sts, sem, peer, ship, ready, open_links):
     nb=32
     one=jnp.ones((),BF); zero=jnp.zeros((),BF)
     iod=lax.broadcasted_iota(I32,(128,256),0).astype(F32).astype(BF)
@@ -47,28 +49,26 @@
     trow=jnp.sum(jnp.where(diag,tot[:,:128],0.),axis=0,keepdims=True)
     tile=jnp.floor(srow*(1/128))
     sh=srow-128.*tile
-    stv[0:1,:]=tile.astype(I32)
-    stv[1:2,:]=jnp.where(sh==0.,0.,128.-sh).astype(I32)
-    stv[2:3,:]=(128.-sh).astype(I32)
-    stv[3:4,:]=trow.astype(I32)
+    stv[0:1,:]=(tile+128.*(128.-sh)+32768.*trow).astype(I32)
     cp=pltpu.make_async_copy(stv,sts,sem)
     cp.start()
     up=(lax.broadcasted_iota(I32,(256,256),0)<lax.broadcasted_iota(I32,(256,256),1)).astype(F32).astype(BF)
-    upones=jnp.concatenate([up,ones],axis=0)
-    lane=lax.broadcasted_iota(I32,(128,256),1).astype(F32)
-    C0=jnp.floor((start+255.-lane)*(1/256)).astype(BF)
-    def ranks(jj,C):
+    first=lax.broadcasted_iota(I32,(256,256),1)==0
+    up=jnp.where(first,1.,up.astype(F32)).astype(BF)
+    lane=lax.broadcasted_iota(I32,(128,256),1)
+    def ranks(jj,base):
         for u in range(PB):
             j=jj*PB+u
             o=oh[j]
-            x=dotf(jnp.concatenate([o,C],axis=1),upones)
-            pos=jnp.sum(o.astype(F32)*x,axis=0,keepdims=True)
+            x=dotf(o,up)
+            b2=jnp.concatenate([base,base],axis=1)
+            pos=jnp.sum(o.astype(F32)*(jnp.where(lane==0,0.,x)+b2),axis=0,keepdims=True)
             hi=jnp.floor(pos*(1/256))
             pos_s[j,0:1,:]=hi
             pos_s[j,1:2,:]=pos-256.*hi
-            C=C+o
-        return C
-    lax.fori_loop(0,nb//PB,ranks,C0)
+            base=base+jnp.broadcast_to(x[:,0:1],(128,128))
+        return base
+    lax.fori_loop(0,nb//PB,ranks,start[:,:128])
     acc[...]=jnp.zeros_like(acc)
     ready()
     iol=lax.broadcasted_iota(I32,(256,256),0).astype(F32).astype(BF)
@@ -107,32 +107,36 @@
             if t-i>=0: csrt[t-i,i:i+1,:]=r
     cp.wait()
     lane=lax.broadcasted_iota(I32,(8,128),1)
-    def expand(k):
-        d=target(k)
-        t=jnp.clip(sts[0,d],0,64); rot=sts[1,d]; thr=sts[2,d]; n=sts[3,d]
+    lane2=lane+128
+    def expand(d):
+        w=sts[0,d]
+        t=w&127; rot=(w>>7)&255; n=w>>15
         rs=[pltpu.roll(srt[t+i],rot,1) for i in range(3)]
         c=pltpu.roll(csrt[t],rot,1)
-        keep=lane<thr
+        keep=lane<rot
         c1=jnp.where(keep[0:2],c[0:2],c[1:3])
-        for i in range(2):
-            live=lane<n-128*i
+        for i,at in enumerate((lane,lane2)):
+            live=at<n
             out[d,:,128*i:128*(i+1)]=jnp.where(live,jnp.where(keep,rs[i],rs[i+1]),0.)
             cells[d,:,128*i:128*(i+1)]=jnp.where(live[0:1],c1[i:i+1],-1.)
-    def back(k):
-        k=k-STRIDE*XB%128
-        return jnp.where(k<0,k+128,k)
-    def deliver(i,k):
-        old=k
-        for u in range(XB):
-            k=turn(k)
-            expand(k)
-        @pl.when(i>0)
-        def _():
-            ship(i-1,back(old),XB)
-        return k
     open_links()
-    k=lax.fori_loop(0,128//XB,deliver,0)
-    ship(128//XB-1,back(k),XB-1)
+    first=peer(0,0)
+    second=wrap(first+STEP)
+    for base in (first,second):
+        for u in range(SB):
+            expand(wrap(base+TURN[u]))
+    ship(0,first,1)
+    def deliver(m,base):
+        now=wrap(base+STEP)
+        for u in range(SB):
+            expand(wrap(now+TURN[u]))
+        ship((m-1)//(U//SB),base,0)
+        return now
+    last=lax.fori_loop(2,128//SB,deliver,second)
+    ship(128//U-1,last,0)
+
+def wrap(p):
+    return jnp.where(p >= 128, p - 128, p)
 
 def split(x):
     h=x.astype(BF); return h,(x-h.astype(F32)).astype(BF)
@@ -226,14 +230,16 @@
     me = gx * 32 + col
     barrier = pltpu.get_barrier_semaphore()
 
-    def wrap(p):
-        return jnp.where(p >= 128, p - 128, p)
-
     def other(k):
         return wrap(me + k)
 
-    def turn(k):
-        return wrap(k + STRIDE)
+    def peer(i, u):
+        return wrap(other(lax.rem(i * (TURN[1] * U), 128)) + TURN[u])
+
+    def origin(i, u):
+        s = me - lax.rem(i * (TURN[1] * U), 128)
+        s = jnp.where(s < 0, s + 128, s) - TURN[u]
+        return jnp.where(s < 0, s + 128, s)
 
     def greet(k, _):
         pl.semaphore_signal(barrier, inc=1, device_id=other(k), device_id_type=LOGICAL)
@@ -270,10 +276,9 @@
         for load in loads[2:]:
             load.wait()
 
-    def ship(group, k, count):
-        for u in range(count):
-            k = turn(k)
-            p = other(k)
+    def ship(group, base, at):
+        for u in range(at, SB):
+            p = wrap(base + TURN[u])
             for src, dst, lane_sem, done in ((send, recv, ss.at[0], ra), (scell, rcell, ss.at[1], rb)):
                 pltpu.make_async_remote_copy(
                     src_ref=src.at[p],
@@ -289,7 +294,7 @@
         for copy in borders:
             copy.start()
 
-    bucket(part, dest, ca, cb, send, scell, oh, pos_s, srt, csrt, acc, stv, sts, sem, other, turn, ship, ready, open_links)
+    bucket(part, dest, ca, cb, send, scell, oh, pos_s, srt, csrt, acc, stv, sts, sem, peer, ship, ready, open_links)
     recv[me] = send[me]
     rcell[me] = scell[me]
 
@@ -311,30 +316,35 @@
         copy.wait_recv()
     masks = [(gx > 0).astype(F32), (gx < 3).astype(F32), (col > 0).astype(F32), (col < 31).astype(F32)]
     setup(vel, halo, fh, fl, tab, masks)
-    last = 128 // U - 1
-    per = U // XB
-
-    def step(i, k):
-        @pl.when(i < last)
-        def _full():
-            for q in range(per):
-                arrived(i * per + q, XB)
-
-        @pl.when(i == last)
-        def _short():
-            for q in range(per):
-                arrived(last * per + q, XB - (q == per - 1))
-
-        for u in range(U):
-            k = turn(k)
-            s = me - k
-            s = jnp.where(s < 0, s + 128, s)
-            cell = rcell[s]
-            out[:, pl.ds(pl.multiple_of(s * 256, 256), 256)] = interp(recv[s], cell, fh, fl, tab)
-            cout[s] = cell.astype(I32)
-        return k
-
-    lax.fori_loop(0, 128 // U, step, 0)
+    def sources(group, count):
+        for q in range(count):
+
+            @pl.when(group + q > 0)
+            def _full():
+                arrived(group + q, U)
+
+            if q == 0:
+
+                @pl.when(group == 0)
+                def _short():
+                    arrived(0, U - 1)
+
+        for q in range(count):
+            for u in range(U):
+                s = origin(group + q, u)
+                cell = rcell[s]
+                out[:, pl.ds(pl.multiple_of(s * 256, 256), 256)] = interp(recv[s], cell, fh, fl, tab)
+                cout[s] = cell.astype(I32)
+
+    done = 0
+    for times, count in STEPS:
+
+        def step(i, _, done=done, count=count):
+            sources(done + i * count, count)
+            return _
+
+        lax.fori_loop(0, times, step, 0)
+        done += times * count
     bytes_of(127, send, recv, ss.at[0], ra.at[0]).wait_send()
     bytes_of(127, scell, rcell, ss.at[1], rb.at[0]).wait_send()
     bytes_of(8, halo, halo, ss.at[2], rh.at[0]).wait_send()
@@ -384,16 +394,16 @@
             pltpu.VMEM((2, 8, 128), F32),
             pltpu.VMEM((32, 128, 256), BF),
             pltpu.VMEM((32, 2, 256), F32),
-            pltpu.VMEM((67, 8, 128), F32),
-            pltpu.VMEM((67, 8, 128), F32),
+            pltpu.VMEM((130, 8, 128), F32),
+            pltpu.VMEM((130, 8, 128), F32),
             pltpu.VMEM((576, 256), F32),
             pltpu.VMEM((8, 128), I32),
             pltpu.SMEM((8, 128), I32),
             pltpu.SemaphoreType.DMA,
             pltpu.SemaphoreType.DMA((5,)),
             pltpu.SemaphoreType.DMA((3,)),
-            pltpu.SemaphoreType.DMA((128 // XB,)),
-            pltpu.SemaphoreType.DMA((128 // XB,)),
+            pltpu.SemaphoreType.DMA((128 // U,)),
+            pltpu.SemaphoreType.DMA((128 // U,)),
             pltpu.SemaphoreType.DMA((8,)),
         ],
         compiler_params=pltpu.CompilerParams(collective_id=0, has_side_effects=True),

time: 37.9 us -> 37.7 us (level)
  no operation moved by 1% of the time
where the time goes in v5:
time: 37.7 us; the launch traced here: 37.6 us
  Pallas kernels  36.9 us (98%)
  between operations  0.64 us (2%)
    pallas_call x1, Pallas kernels, shards(): pl.pallas_call(fused, out_shape=(pltpu.VMEM((8, 32768), F32), pltpu.VMEM(...  35.9 us
    pallas_call x1, Pallas kernels, settle(): pl.pallas_call(put_out, out_shape=(jax.ShapeDtypeStruct(binned.shape, F32...  1.02 us

profile of v5, /device:TPU:1, one launch (start us, length us, event | category | flops | bytes accessed | tf_op | source)
XLA Modules:
  0.0 37.6 jit_solution(8060078824797128943)
XLA Ops:
  0.6 35.9 %rebin.1 = (f32[8,32768]{1,0:T(8,128)S(1)}, s32[128,1,256]{2,1,0:T(1,128)S(1)}) custom-call(f32[2,256,128]{2,1,0:T(8,128)} %vel_in.1, f32[8,8192]{1,0:T(8,128)} %part_in.1, s32[64,128]{1,0:T(8,128)} %bitcast.4, s32[64,128]{1,0:T(8,128)} %bitcast.5, s32[64,128]{1,0:T(8,128)} %bitcast.6), custom_call_target="tpu_custom_call" | custom-call | tf_op jit(solution)/shard_map/rebin/pallas_call | solution.py:375
  36.5 1.0 %settle.1 = (f32[8,32768]{1,0:T(8,128)}, s32[128,1,256]{2,1,0:T(1,128)}) custom-call(f32[8,32768]{1,0:T(8,128)S(1)} %get-tuple-element.6.a_ref, s32[128,1,256]{2,1,0:T(1,128)S(1)} %get-tuple-element.7.b_ref), custom_call_target="tpu_custom_call" | custom-call | tf_op jit(solution)/shard_map/settle/pallas_call | solution.py:362

commit v6 on v5

--- a/solution.py
+++ b/solution.py
@@ -18,8 +18,8 @@
     return jnp.dot(a, b, preferred_element_type=F32)
 
 
-PB=16
-UB=16
+PB=32
+UB=32
 U=16
 STEPS=((4,1),(2,2))
 SB=8
@@ -68,8 +68,7 @@
             pos_s[j,1:2,:]=pos-256.*hi
             base=base+jnp.broadcast_to(x[:,0:1],(128,128))
         return base
-    lax.fori_loop(0,nb//PB,ranks,start[:,:128])
-    acc[...]=jnp.zeros_like(acc)
+    ranks(0,start[:,:128])
     ready()
     iol=lax.broadcasted_iota(I32,(256,256),0).astype(F32).astype(BF)
     s16=lax.broadcasted_iota(I32,(16,256),0)
@@ -81,7 +80,7 @@
             j=jj*UB+u
             hi=pos_s[j,0:1,:].astype(BF); lo=pos_s[j,1:2,:].astype(BF)
             lot=jnp.where(iol==jnp.broadcast_to(lo,(256,256)),one,zero)
-            v=part[:,pl.ds(pl.multiple_of(j*256,256),256)]
+            v=part[:,j*256:(j+1)*256]
             vh=v.astype(BF).astype(F32); vl=v-vh
             vh2=jnp.concatenate([vh,vh],axis=0).astype(BF)
             vl2=jnp.concatenate([vl,vl],axis=0).astype(BF)
@@ -94,9 +93,9 @@
             a=row256(ca,j).astype(F32).astype(BF); b=row256(cb,j).astype(F32).astype(BF)
             As.append(jnp.concatenate(hs+ls+[jnp.where(m32,jnp.broadcast_to(a,(32,256)),zero),jnp.where(m32,jnp.broadcast_to(b,(32,256)),zero)],axis=0))
             Ls.append(lot)
-        acc[...]+=lax.dot_general(jnp.concatenate(As,axis=1),jnp.concatenate(Ls,axis=1),NT,preferred_element_type=F32)
+        acc[...]=lax.dot_general(jnp.concatenate(As,axis=1),jnp.concatenate(Ls,axis=1),NT,preferred_element_type=F32)
         return _
-    lax.fori_loop(0,nb//UB,place,0)
+    place(0,0)
     for h in range(32):
         x=acc[h*8:(h+1)*8]+acc[256+h*8:256+(h+1)*8]
         srt[2*h]=x[:,:128]; srt[2*h+1]=x[:,128:]

time: 37.7 us -> 37 us (0.981)
  Pallas kernels: 36.9 us -> 36.3 us
    pallas_call x1, Pallas kernels: 35.9 us -> 35.3 us  [shards(): pl.pallas_call(fused, out_shape=(pltpu.VMEM((8, 32768), F32), pltpu.VMEM(...]
where the time goes in v6:
time: 37 us; the launch traced here: 36.9 us
  Pallas kernels  36.3 us (98%)
  between operations  0.64 us (2%)
    pallas_call x1, Pallas kernels, shards(): pl.pallas_call(fused, out_shape=(pltpu.VMEM((8, 32768), F32), pltpu.VMEM(...  35.3 us
    pallas_call x1, Pallas kernels, settle(): pl.pallas_call(put_out, out_shape=(jax.ShapeDtypeStruct(binned.shape, F32...  1.02 us

profile of v6, /device:TPU:1, one launch (start us, length us, event | category | flops | bytes accessed | tf_op | source)
XLA Modules:
  0.0 36.9 jit_solution(14568451538262892041)
XLA Ops:
  0.6 35.3 %rebin.1 = (f32[8,32768]{1,0:T(8,128)S(1)}, s32[128,1,256]{2,1,0:T(1,128)S(1)}) custom-call(f32[2,256,128]{2,1,0:T(8,128)} %vel_in.1, f32[8,8192]{1,0:T(8,128)} %part_in.1, s32[64,128]{1,0:T(8,128)} %bitcast.4, s32[64,128]{1,0:T(8,128)} %bitcast.5, s32[64,128]{1,0:T(8,128)} %bitcast.6), custom_call_target="tpu_custom_call" | custom-call | tf_op jit(solution)/shard_map/rebin/pallas_call | solution.py:374
  35.9 1.0 %settle.1 = (f32[8,32768]{1,0:T(8,128)}, s32[128,1,256]{2,1,0:T(1,128)}) custom-call(f32[8,32768]{1,0:T(8,128)S(1)} %get-tuple-element.6.a_ref, s32[128,1,256]{2,1,0:T(1,128)S(1)} %get-tuple-element.7.b_ref), custom_call_target="tpu_custom_call" | custom-call | tf_op jit(solution)/shard_map/settle/pallas_call | solution.py:361

commit v7 on v6

--- a/solution.py
+++ b/solution.py
@@ -240,11 +240,8 @@
         s = jnp.where(s < 0, s + 128, s) - TURN[u]
         return jnp.where(s < 0, s + 128, s)
 
-    def greet(k, _):
+    for k in range(1, 128):
         pl.semaphore_signal(barrier, inc=1, device_id=other(k), device_id_type=LOGICAL)
-        return _
-
-    lax.fori_loop(1, 128, greet, 0)
     loads[0].wait()
     loads[1].wait()
     for c in range(2):

time: 37 us -> 36.7 us (level)
  Pallas kernels: 36.3 us -> 35.9 us
    pallas_call x1, Pallas kernels: 35.3 us -> 34.9 us  [shards(): pl.pallas_call(fused, out_shape=(pltpu.VMEM((8, 32768), F32), pltpu.VMEM(...]
where the time goes in v7:
time: 36.7 us; the launch traced here: 36.6 us
  Pallas kernels  35.9 us (98%)
  between operations  0.64 us (2%)
    pallas_call x1, Pallas kernels, shards(): pl.pallas_call(fused, out_shape=(pltpu.VMEM((8, 32768), F32), pltpu.VMEM(...  34.9 us
    pallas_call x1, Pallas kernels, settle(): pl.pallas_call(put_out, out_shape=(jax.ShapeDtypeStruct(binned.shape, F32...  1.02 us

profile of v7, /device:TPU:1, one launch (start us, length us, event | category | flops | bytes accessed | tf_op | source)
XLA Modules:
  0.0 36.6 jit_solution(14129471937001761597)
XLA Ops:
  0.6 34.9 %rebin.1 = (f32[8,32768]{1,0:T(8,128)S(1)}, s32[128,1,256]{2,1,0:T(1,128)S(1)}) custom-call(f32[2,256,128]{2,1,0:T(8,128)} %vel_in.1, f32[8,8192]{1,0:T(8,128)} %part_in.1, s32[64,128]{1,0:T(8,128)} %bitcast.4, s32[64,128]{1,0:T(8,128)} %bitcast.5, s32[64,128]{1,0:T(8,128)} %bitcast.6), custom_call_target="tpu_custom_call" | custom-call | tf_op jit(solution)/shard_map/rebin/pallas_call | solution.py:371
  35.5 1.0 %settle.1 = (f32[8,32768]{1,0:T(8,128)}, s32[128,1,256]{2,1,0:T(1,128)}) custom-call(f32[8,32768]{1,0:T(8,128)S(1)} %get-tuple-element.6.a_ref, s32[128,1,256]{2,1,0:T(1,128)S(1)} %get-tuple-element.7.b_ref), custom_call_target="tpu_custom_call" | custom-call | tf_op jit(solution)/shard_map/settle/pallas_call | solution.py:358
